TPU v7x, 512 devices: a whole 4x8x8 slice. The times are simulated.
512 devices in a mesh: pool: 16 (over z, y_hi), fft: 32 (over x, y_lo, core).
Axes of the slice: x: 4, y: 8 (y_hi: 2, y_lo: 4; y = y_hi * 4 + y_lo), z: 8, core: 2. Of those that a mesh axis runs over, the one named last changes fastest.
Arguments:
- orbitals: bfloat16 [16, 2, 1, 160, 25600], P('pool', None, None, 'fft'), may hold values from -6 to 6
- stick_map: int32 [16000], replicated, may hold values from -1 to 25599, as said below
- kpoint_grid: int32 [16, 3], replicated, may hold values from 0 to 3, as said below
Outputs:
- exchange_action: bfloat16 [16, 2, 1, 160, 25600], P('pool', None, None, 'fft')
Inputs may be any that keep to these rules, and one draw needn't show every extreme that they name: `stick_map`: entries other than -1 are distinct columns. Slots come in blocks of 500 per index of fft; in each block at least half of the slots are live, and in every draw some block has all 500 live. `kpoint_grid`: rows are distinct.
All inputs are finite; a program needn't handle non-finite values.
Results may differ from a plain program's by a relative error of at most 0.011.
Values may be sent and summed in bfloat16 or wider, within the bound.
A program may use at most 64 MiB of HBM per device.

v0:
```python
import math

import jax
import jax.numpy as jnp
from jax import lax
from jax.sharding import PartitionSpec as P

NG = 160
KMESH = 4


SPACING_BOHR = 0.1875
SCREENING = 0.106


def shifted(value, axis, steps):
    count = lax.axis_size(axis)
    pairs = [(source, (source + steps) % count) for source in range(count)]
    return lax.ppermute(value, axis, pairs)


def dft_table(grid_size, orientation):
    positions = jnp.arange(grid_size, dtype=jnp.int32)
    product = positions[:, None] * positions[None, :] % grid_size
    angle = product.astype(jnp.float32) * (2.0 * math.pi / grid_size)
    cosine = jnp.cos(angle)
    sine = orientation * jnp.sin(angle)
    upper = jnp.stack([cosine, sine], axis=1)
    lower = jnp.stack([-sine, cosine], axis=1)
    return jnp.stack([upper, lower], axis=0).astype(jnp.bfloat16)


def signed(frequency, grid_size):
    return jnp.where(frequency >= grid_size // 2, frequency - grid_size, frequency)


def kernel_table(columns, shift_q, grid_size):
    live_slot = columns >= 0
    column_ids = jnp.where(live_slot, columns, 0)
    freq_x = signed(column_ids % grid_size, grid_size)
    freq_y = signed(column_ids // grid_size, grid_size)
    freq_z = signed(jnp.arange(grid_size, dtype=jnp.int32), grid_size)
    radius = grid_size // 2
    inside = (freq_x * freq_x + freq_y * freq_y)[None, :] + (freq_z * freq_z)[
        :, None
    ] <= radius * radius
    inside = jnp.logical_and(inside, live_slot[None, :])
    wave_x = freq_x.astype(jnp.float32) + shift_q[0]
    wave_y = freq_y.astype(jnp.float32) + shift_q[1]
    wave_z = freq_z.astype(jnp.float32) + shift_q[2]
    square = (wave_z * wave_z)[:, None] + (wave_x * wave_x + wave_y * wave_y)[None, :]
    cell = SPACING_BOHR * grid_size
    exponent = math.pi * math.pi * square / (cell * cell * SCREENING * SCREENING)
    weights = cell * cell / math.pi * -jnp.expm1(-exponent) / square / float(grid_size) ** 3
    return jnp.where(inside, weights, 0.0)


def momentum(kpoint_grid, pool_rank, pool_count):
    pool_rows = jnp.arange(pool_count, dtype=jnp.int32)
    earlier = (pool_rank + pool_count - 1) % pool_count
    current = jnp.sum(jnp.where((pool_rows == pool_rank)[:, None], kpoint_grid, 0), axis=0)
    previous = jnp.sum(jnp.where((pool_rows == earlier)[:, None], kpoint_grid, 0), axis=0)
    return (current - previous).astype(jnp.float32) / KMESH


def pair_density(own_bands, received):
    band_count = own_bands.shape[1]
    real_own = own_bands[0].astype(jnp.float32)[:, None]
    imag_own = own_bands[1].astype(jnp.float32)[:, None]
    real_recv = received[0].astype(jnp.float32)[None]
    imag_recv = received[1].astype(jnp.float32)[None]
    real_part = real_recv * real_own + imag_recv * imag_own
    imag_part = real_recv * imag_own - imag_recv * real_own
    stacked = jnp.stack([real_part, imag_part], axis=2)
    return stacked.reshape((band_count * band_count, 2) + own_bands.shape[2:]).astype(jnp.bfloat16)


def action_of(received, field):
    band_count = received.shape[1]
    field = field.reshape((band_count, band_count) + field.shape[1:])
    real_recv = received[0].astype(jnp.float32)[None]
    imag_recv = received[1].astype(jnp.float32)[None]
    real_field = field[:, :, 0]
    imag_field = field[:, :, 1]
    real_part = -jnp.sum(real_recv * real_field - imag_recv * imag_field, axis=1)
    imag_part = -jnp.sum(real_recv * imag_field + imag_recv * real_field, axis=1)
    return jnp.stack([real_part, imag_part], axis=0).astype(jnp.bfloat16)


def apply_table(data, table, form):
    return jnp.einsum(form, data, table, preferred_element_type=jnp.float32)


def column_pass(picked, weights, forward, backward):
    spectrum = apply_table(picked, forward, "pczs,czdk->pdks")
    scaled = (spectrum * weights).astype(jnp.bfloat16)
    return apply_table(scaled, backward, "pczs,czdk->pdks").astype(jnp.bfloat16)


def local(orbitals, stick_map, kpoint_grid):
    grid_size = NG
    moved = shifted(orbitals, "pool", 1)
    own_bands = orbitals[0].reshape(orbitals.shape[1:4] + (grid_size, grid_size))
    received = moved[0].reshape(orbitals.shape[1:4] + (grid_size, grid_size))
    fft_count = lax.axis_size("fft")
    fft_rank = lax.axis_index("fft")
    pool_count = lax.axis_size("pool")
    pool_rank = lax.axis_index("pool")
    shift_q = momentum(kpoint_grid, pool_rank, pool_count)
    forward = dft_table(grid_size, -1.0)
    backward = dft_table(grid_size, 1.0)
    column_share = grid_size * grid_size // fft_count
    share_ids = fft_rank * column_share + jnp.arange(column_share, dtype=jnp.int32)
    ordered_map = jnp.sort(stick_map)
    found_at = jnp.searchsorted(ordered_map, share_ids)
    found_at = jnp.minimum(found_at, stick_map.shape[0] - 1)
    own_present = jnp.take(ordered_map, found_at) == share_ids
    weights = kernel_table(jnp.where(own_present, share_ids, -1), shift_q, grid_size)

    def potential(pair_block):
        along_x = apply_table(pair_block, forward, "pczyx,cxek->pezyk").astype(jnp.bfloat16)
        along_y = apply_table(along_x, forward, "pczyx,cyek->pezkx").astype(jnp.bfloat16)
        piece_block = lax.all_to_all(along_y, "fft", split_axis=3, concat_axis=2, tiled=True)
        flat_piece = piece_block.reshape(piece_block.shape[:3] + (column_share,))
        scaled_back = column_pass(flat_piece, weights, forward, backward).reshape(piece_block.shape)
        spectrum = lax.all_to_all(scaled_back, "fft", split_axis=2, concat_axis=3, tiled=True)
        back_y = apply_table(spectrum, backward, "pczkx,ckey->pezyx").astype(jnp.bfloat16)
        return apply_table(back_y, backward, "pczyk,ckex->pezyx")

    density = pair_density(own_bands, received)
    field = lax.map(lambda single_pair: potential(single_pair[None])[0], density)
    result = action_of(received, field)
    return result.reshape((1,) + result.shape[:3] + (grid_size * grid_size,))


def solution(mesh):
    return jax.shard_map(
        local,
        mesh=mesh,
        in_specs=(P("pool", None, None, "fft", None), P(), P()),
        out_specs=P("pool", None, None, "fft", None),
        check_vma=False,
    )
```

profile of v0, /device:TPU:1, one launch (start us, length us, event | category | flops | bytes accessed | tf_op | source)
XLA Modules:
  0.0 173.2 jit_solution(10749777014005598855)
XLA Ops:
  0.0 8.3 %collective-permute-start = (bf16[1,2,1,5,25600]{4,1,3,2,0:T(2,128)(2,1)}, bf16[1,2,1,5,25600]{4,1,3,2,0:T(2,128)(2,1)S(1)}, u32[]{:S(2)}, u32[]{:S(2)}) collective-permute-start(bf16[1,2,1,5,25600]{4,1,3,2,0:T(2,128)(2,1)} %param.5), channel_id=1, source_target_pairs={{0,32},{32,64},{64,96},{96,128},{128,160},{160,192},{192,224},{224... | collective-permute-start | bytes 1536008 | tf_op jit(solution)/shard_map/ppermute | solution.py:19
  9.8 8.6 %sort.15 = (s32[16000]{0:T(1024)S(1)}, s32[16000]{0:T(1024)}) sort(s32[16000]{0:T(1024)} %param.6, s32[16000]{0:T(1024)S(1)} %iota.64), dimensions={0}, to_apply=%region_0.1 | sort | flops 224000 | bytes 256000 | tf_op jit(solution)/shard_map/jit(sort)/sort | solution.py:114
  18.4 69.4 %while.28 = (s32[]{:T(128)}, u32[800]{0:T(1024)S(1)}, u32[800]{0:T(1024)S(1)}, s32[16000]{0:T(1024)S(1)}, s32[]{:T(128)}, /*index=5*/s32[]{:T(128)}, s32[]{:T(128)}, s32[]{}) while((s32[]{:T(128)}, u32[800]{0:T(1024)S(1)}, u32[800]{0:T(1024)S(1)}, s32[16000]{0:T(1024)S(1)}, s32[]{:T(128)}, /*index=5*/s32[]{:T(128)}, s32[]{:T(128)}, ...), condition=%wide.region_2.3_spmd.clone, body=%wide.region_1.2_spmd.clone.sunk | while | flops 16228 | bytes 57017 | solution.py:115
  18.4 4.9 %gather_fusion = s32[800]{0:T(1024)S(1)} fusion(s32[16000]{0:T(1024)S(1)} %get-tuple-element.202, u32[1024]{0:T(1024)S(1)} %pad_clamp_fusion.3), kind=kCustom, calls=%fused_computation.clone.clone.1 | custom fusion | bytes 9600 | tf_op jit(solution)/shard_map/jit(searchsorted)/jit(_searchsorted_scan_impl)/vmap(jit(_searchsorted_scan_impl))/while/body/eval_jaxpr/gather | solution.py:115
  23.4 4.9 %gather_fusion = s32[800]{0:T(1024)S(1)} fusion(s32[16000]{0:T(1024)S(1)} %get-tuple-element.202, u32[1024]{0:T(1024)S(1)} %pad_clamp_fusion.3), kind=kCustom, calls=%fused_computation.clone.clone.1 | custom fusion | bytes 9600 | tf_op jit(solution)/shard_map/jit(searchsorted)/jit(_searchsorted_scan_impl)/vmap(jit(_searchsorted_scan_impl))/while/body/eval_jaxpr/gather | solution.py:115
  28.4 4.9 %gather_fusion = s32[800]{0:T(1024)S(1)} fusion(s32[16000]{0:T(1024)S(1)} %get-tuple-element.202, u32[1024]{0:T(1024)S(1)} %pad_clamp_fusion.3), kind=kCustom, calls=%fused_computation.clone.clone.1 | custom fusion | bytes 9600 | tf_op jit(solution)/shard_map/jit(searchsorted)/jit(_searchsorted_scan_impl)/vmap(jit(_searchsorted_scan_impl))/while/body/eval_jaxpr/gather | solution.py:115
  33.3 4.9 %gather_fusion = s32[800]{0:T(1024)S(1)} fusion(s32[16000]{0:T(1024)S(1)} %get-tuple-element.202, u32[1024]{0:T(1024)S(1)} %pad_clamp_fusion.3), kind=kCustom, calls=%fused_computation.clone.clone.1 | custom fusion | bytes 9600 | tf_op jit(solution)/shard_map/jit(searchsorted)/jit(_searchsorted_scan_impl)/vmap(jit(_searchsorted_scan_impl))/while/body/eval_jaxpr/gather | solution.py:115
  38.3 4.9 %gather_fusion = s32[800]{0:T(1024)S(1)} fusion(s32[16000]{0:T(1024)S(1)} %get-tuple-element.202, u32[1024]{0:T(1024)S(1)} %pad_clamp_fusion.3), kind=kCustom, calls=%fused_computation.clone.clone.1 | custom fusion | bytes 9600 | tf_op jit(solution)/shard_map/jit(searchsorted)/jit(_searchsorted_scan_impl)/vmap(jit(_searchsorted_scan_impl))/while/body/eval_jaxpr/gather | solution.py:115
  43.2 4.9 %gather_fusion = s32[800]{0:T(1024)S(1)} fusion(s32[16000]{0:T(1024)S(1)} %get-tuple-element.202, u32[1024]{0:T(1024)S(1)} %pad_clamp_fusion.3), kind=kCustom, calls=%fused_computation.clone.clone.1 | custom fusion | bytes 9600 | tf_op jit(solution)/shard_map/jit(searchsorted)/jit(_searchsorted_scan_impl)/vmap(jit(_searchsorted_scan_impl))/while/body/eval_jaxpr/gather | solution.py:115
  48.2 4.9 %gather_fusion = s32[800]{0:T(1024)S(1)} fusion(s32[16000]{0:T(1024)S(1)} %get-tuple-element.202, u32[1024]{0:T(1024)S(1)} %pad_clamp_fusion.3), kind=kCustom, calls=%fused_computation.clone.clone.1 | custom fusion | bytes 9600 | tf_op jit(solution)/shard_map/jit(searchsorted)/jit(_searchsorted_scan_impl)/vmap(jit(_searchsorted_scan_impl))/while/body/eval_jaxpr/gather | solution.py:115
  53.1 4.9 %gather_fusion = s32[800]{0:T(1024)S(1)} fusion(s32[16000]{0:T(1024)S(1)} %get-tuple-element.202, u32[1024]{0:T(1024)S(1)} %pad_clamp_fusion.3), kind=kCustom, calls=%fused_computation.clone.clone.1 | custom fusion | bytes 9600 | tf_op jit(solution)/shard_map/jit(searchsorted)/jit(_searchsorted_scan_impl)/vmap(jit(_searchsorted_scan_impl))/while/body/eval_jaxpr/gather | solution.py:115
  58.1 4.9 %gather_fusion = s32[800]{0:T(1024)S(1)} fusion(s32[16000]{0:T(1024)S(1)} %get-tuple-element.202, u32[1024]{0:T(1024)S(1)} %pad_clamp_fusion.3), kind=kCustom, calls=%fused_computation.clone.clone.1 | custom fusion | bytes 9600 | tf_op jit(solution)/shard_map/jit(searchsorted)/jit(_searchsorted_scan_impl)/vmap(jit(_searchsorted_scan_impl))/while/body/eval_jaxpr/gather | solution.py:115
  63.1 4.9 %gather_fusion = s32[800]{0:T(1024)S(1)} fusion(s32[16000]{0:T(1024)S(1)} %get-tuple-element.202, u32[1024]{0:T(1024)S(1)} %pad_clamp_fusion.3), kind=kCustom, calls=%fused_computation.clone.clone.1 | custom fusion | bytes 9600 | tf_op jit(solution)/shard_map/jit(searchsorted)/jit(_searchsorted_scan_impl)/vmap(jit(_searchsorted_scan_impl))/while/body/eval_jaxpr/gather | solution.py:115
  68.0 4.9 %gather_fusion = s32[800]{0:T(1024)S(1)} fusion(s32[16000]{0:T(1024)S(1)} %get-tuple-element.202, u32[1024]{0:T(1024)S(1)} %pad_clamp_fusion.3), kind=kCustom, calls=%fused_computation.clone.clone.1 | custom fusion | bytes 9600 | tf_op jit(solution)/shard_map/jit(searchsorted)/jit(_searchsorted_scan_impl)/vmap(jit(_searchsorted_scan_impl))/while/body/eval_jaxpr/gather | solution.py:115
  73.0 4.9 %gather_fusion = s32[800]{0:T(1024)S(1)} fusion(s32[16000]{0:T(1024)S(1)} %get-tuple-element.202, u32[1024]{0:T(1024)S(1)} %pad_clamp_fusion.3), kind=kCustom, calls=%fused_computation.clone.clone.1 | custom fusion | bytes 9600 | tf_op jit(solution)/shard_map/jit(searchsorted)/jit(_searchsorted_scan_impl)/vmap(jit(_searchsorted_scan_impl))/while/body/eval_jaxpr/gather | solution.py:115
  77.9 4.9 %gather_fusion = s32[800]{0:T(1024)S(1)} fusion(s32[16000]{0:T(1024)S(1)} %get-tuple-element.202, u32[1024]{0:T(1024)S(1)} %pad_clamp_fusion.3), kind=kCustom, calls=%fused_computation.clone.clone.1 | custom fusion | bytes 9600 | tf_op jit(solution)/shard_map/jit(searchsorted)/jit(_searchsorted_scan_impl)/vmap(jit(_searchsorted_scan_impl))/while/body/eval_jaxpr/gather | solution.py:115
  82.9 4.9 %gather_fusion = s32[800]{0:T(1024)S(1)} fusion(s32[16000]{0:T(1024)S(1)} %get-tuple-element.202, u32[1024]{0:T(1024)S(1)} %pad_clamp_fusion.3), kind=kCustom, calls=%fused_computation.clone.clone.1 | custom fusion | bytes 9600 | tf_op jit(solution)/shard_map/jit(searchsorted)/jit(_searchsorted_scan_impl)/vmap(jit(_searchsorted_scan_impl))/while/body/eval_jaxpr/gather | solution.py:115
  87.9 4.9 %gather_fusion.1 = s32[800]{0:T(1024)S(1)} fusion(s32[16000]{0:T(1024)S(1)} %get-tuple-element.207, s32[1024]{0:T(1024)S(1)} %pad_clamp_fusion.1), kind=kCustom, calls=%fused_computation.1 | custom fusion | bytes 9600 | tf_op jit(solution)/shard_map/jit(_take)/gather | solution.py:117
  94.9 4.1 %fusion.34 = (bf16[5,25600]{1,0:T(8,128)(2,1)S(1)}, bf16[5,25600]{1,0:T(8,128)(2,1)S(1)}) fusion(bf16[1,2,1,5,25600]{4,1,3,2,0:T(2,128)(2,1)S(1)} %copy-done, bf16[1,2,1,5,25600]{4,1,3,2,0:T(2,128)(2,1)S(1)} %collective-permute-done), kind=kLoop, calls=%fused_computation.57 | loop fusion | flops 1536000 | bytes 1536000 | tf_op jit(solution)/shard_map/convert.5
  102.9 5.8 %all-to-all-start = ((bf16[1,2,5,160,160]{4,1,2,0,3:T(2,128)(2,1)}), bf16[1,2,5,160,160]{4,1,2,0,3:T(2,128)(2,1)S(1)}, u32[]{:S(2)}, u32[]{:S(2)}) async-start(bf16[1,2,5,160,160]{4,1,2,0,3:T(2,128)(2,1)} %copy.79), calls=%async_computation | async-start | bytes 1638400 | tf_op jit(solution)/shard_map/while/body/eval_jaxpr/all_to_all | solution.py:123
  111.1 20.5 %all-to-all-done = bf16[1,2,5,160,160]{4,1,2,0,3:T(2,128)(2,1)S(1)} async-done(((bf16[1,2,5,160,160]{4,1,2,0,3:T(2,128)(2,1)}), bf16[1,2,5,160,160]{4,1,2,0,3:T(2,128)(2,1)S(1)}, u32[]{:S(2)}, u32[]{:S(2)}) %all-to-all-start) | async-done | bytes 512032 | tf_op jit(solution)/shard_map/while/body/eval_jaxpr/all_to_all | solution.py:123
  133.4 1.8 %fusion.4 = bf16[2,160,800]{2,1,0:T(8,128)(2,1)S(1)} fusion(bf16[2,160,800,1]{2,1,0,3:T(8,128)(2,1)S(1)} %reshape.578, f32[160,800]{1,0:T(8,128)S(1)} %fusion.20, bf16[1,160,2,160]{1,3,0,2:T(8,128)(2,1)S(1)} %get-tuple-element.136, bf16[1,160,2,160]{1,3,0,2:T(8,128)(2,1)} %copy-done.1, bf16[1,160,2,160]{1,3,2,0:T(8,128)(2,1)S(1)} %get-tuple-element.138, ...), kind=kOutput, calls=%fused_computation.16 | convolution fusion | flops 328652800 | bytes 1945600 | tf_op jit(solution)/shard_map/while/body/eval_jaxpr/pczs,czdk->pdks/dot_general | solution.py:91
  137.2 26.6 %all_to_all.38 = bf16[1,2,160,5,160]{4,1,3,0,2:T(2,128)(2,1)S(1)} all-to-all(bf16[1,2,160,5,160]{4,1,3,0,2:T(2,128)(2,1)S(1)} %copy.83), channel_id=1, replica_groups=mesh['pool'=16,'fft'=32] {'fft'}, dimensions={2} | all-to-all | bytes 1024000 | tf_op jit(solution)/shard_map/while/body/eval_jaxpr/all_to_all | solution.py:126
  168.4 1.8 %negate_convert_fusion.1 = (bf16[1,1,1,5,25600]{4,2,3,1,0:T(2,128)(2,1)S(1)}, bf16[1,1,1,5,25600]{4,2,3,1,0:T(2,128)(2,1)S(1)}) fusion(f32[1,1,1,5,25600]{4,2,3,1,0:T(1,128)S(1)} %squeeze.35, f32[1,1,1,5,25600]{4,2,3,1,0:T(1,128)S(1)} %squeeze.34, bf16[1,2,1,5,25600]{4,1,3,2,0:T(2,128)(2,1)S(1)} %collective-permute-done), kind=kLoop, calls=%fused_computation.55 | loop fusion | flops 1536000 | bytes 2048000 | tf_op jit(solution)/shard_map/convert
  (113 shorter events, 21.8 us)
Async XLA Ops:
  0.0 94.8 %collective-permute-start = (bf16[1,2,1,5,25600]{4,1,3,2,0:T(2,128)(2,1)}, bf16[1,2,1,5,25600]{4,1,3,2,0:T(2,128)(2,1)S(1)}, u32[]{:S(2)}, u32[]{:S(2)}) collective-permute-start(bf16[1,2,1,5,25600]{4,1,3,2,0:T(2,128)(2,1)} %param.5), channel_id=1, source_target_pairs={{0,32},{32,64},{64,96},{96,128},{128,160},{160,192},{192,224},{224... | collective-permute-start | bytes 1536008 | tf_op jit(solution)/shard_map/ppermute | solution.py:19
  92.7 2.1 %copy-start = (bf16[1,2,1,5,25600]{4,1,3,2,0:T(2,128)(2,1)S(1)}, bf16[1,2,1,5,25600]{4,1,3,2,0:T(2,128)(2,1)}, u32[]{:S(2)}) copy-start(bf16[1,2,1,5,25600]{4,1,3,2,0:T(2,128)(2,1)} %param.5) | copy-start | bytes 1536004
  94.8 8.0 %copy-start.1 = (bf16[1,160,2,160]{1,3,0,2:T(8,128)(2,1)}, bf16[1,160,2,160]{1,3,0,2:T(8,128)(2,1)S(1)}, u32[]{:S(2)}) copy-start(bf16[1,160,2,160]{1,3,0,2:T(8,128)(2,1)S(1)} %get-tuple-element.137) | copy-start | bytes 307204
  102.9 28.8 %all-to-all-start = ((bf16[1,2,5,160,160]{4,1,2,0,3:T(2,128)(2,1)}), bf16[1,2,5,160,160]{4,1,2,0,3:T(2,128)(2,1)S(1)}, u32[]{:S(2)}, u32[]{:S(2)}) async-start(bf16[1,2,5,160,160]{4,1,2,0,3:T(2,128)(2,1)} %copy.79), calls=%async_computation | async-start | bytes 1638400 | tf_op jit(solution)/shard_map/while/body/eval_jaxpr/all_to_all | solution.py:123
where the time goes:
time: 174 us; the launch traced here: 173 us
  local copies, waits for them, and re-layouts  84.9 us (49%)
  blocking collectives  26.6 us (15%)
  other arithmetic  22.1 us (13%)
  waiting for transfers between devices  20.5 us (12%)
  starting transfers between devices  14 us (8%)
  matrix products  4.07 us (2%)
    gather x14, local copies, waits for them, and re-layouts, local(): found_at = jnp.searchsorted(ordered_map, share_ids)  68.1 us
    all_to_all x1, blocking collectives, potential(): lax.all_to_all(scaled_back, 'fft', split_axis=2, concat_axis=3, tiled=True)  26.6 us
    all_to_all x1, waiting for transfers between devices, potential(): lax.all_to_all(along_y, 'fft', split_axis=3, concat_axis=2, tiled=True)  20.5 us
    sort x1, other arithmetic, local(): ordered_map = jnp.sort(stick_map)  8.6 us
    ppermute x1, starting transfers between devices, shifted(): return lax.ppermute(value, axis, pairs)  8.26 us
    another operation x5, other arithmetic  7.91 us
    all_to_all x1, starting transfers between devices, potential(): lax.all_to_all(along_y, 'fft', split_axis=3, concat_axis=2, tiled=True)  5.75 us
    gather x1, local copies, waits for them, and re-layouts, local(): own_present = jnp.take(ordered_map, found_at) == share_ids  4.86 us
  transfers between devices with their start and end apart: 2, of which 1 were waited for; matrix products, arithmetic and copies ran while one was open for 51% of the time, Pallas kernels for 0%

commit v1 on v0

--- a/solution.py
+++ b/solution.py
@@ -111,10 +111,17 @@
     backward = dft_table(grid_size, 1.0)
     column_share = grid_size * grid_size // fft_count
     share_ids = fft_rank * column_share + jnp.arange(column_share, dtype=jnp.int32)
-    ordered_map = jnp.sort(stick_map)
-    found_at = jnp.searchsorted(ordered_map, share_ids)
-    found_at = jnp.minimum(found_at, stick_map.shape[0] - 1)
-    own_present = jnp.take(ordered_map, found_at) == share_ids
+    own_rows = fft_rank * (grid_size // fft_count) + jnp.arange(grid_size // fft_count, dtype=jnp.int32)
+    row_hit = (stick_map[None, :] // grid_size == own_rows[:, None]) & (stick_map >= 0)[None, :]
+    every_column = jnp.arange(grid_size, dtype=jnp.int32)
+    column_hit = stick_map[None, :] % grid_size == every_column[:, None]
+    counts = jnp.einsum(
+        "rs,cs->rc",
+        row_hit.astype(jnp.bfloat16),
+        column_hit.astype(jnp.bfloat16),
+        preferred_element_type=jnp.float32,
+    )
+    own_present = counts.reshape(column_share) > 0.5
     weights = kernel_table(jnp.where(own_present, share_ids, -1), shift_q, grid_size)
 
     def potential(pair_block):

time: 174 us -> 118 us (0.68)
  local copies, waits for them, and re-layouts: 84.9 us -> 12.1 us
  waiting for transfers between devices: 20.5 us -> 36.6 us
  starting transfers between devices: 14 us -> 21.7 us
  other arithmetic: 22.1 us -> 14.8 us
  matrix products: 4.07 us -> 5.98 us
    gather x15 -> x0, local copies, waits for them, and re-layouts: 73 us -> none  [the longest x14 68.1 us: local(): found_at = jnp.searchsorted(ordered_map, share_ids)]
    ppermute x1, waiting for transfers between devices: 0.01 us -> 16.1 us  [shifted(): return lax.ppermute(value, axis, pairs)]
    sort x1 -> x0, other arithmetic: 8.6 us -> none  [local(): ordered_map = jnp.sort(stick_map)]
    all_to_all x1, starting transfers between devices: 5.75 us -> 13.5 us  [potential(): lax.all_to_all(along_y, 'fft', split_axis=3, concat_axis=2, tiled=True)]
    dot_general x0 -> x1, matrix products: none -> 1.91 us  [local(): jnp.einsum('rs,cs->rc', row_hit.astype(jnp.bfloat16), column_hit.astype(j...]
  transfers between devices with their start and end apart: 2 -> 2, of which waited for: 1 -> 2; matrix products, arithmetic and copies ran while one was open for 51% -> 8% of each run, Pallas kernels for 0% -> 0%
where the time goes in v1:
time: 118 us
  waiting for transfers between devices  36.6 us (31%)
  blocking collectives  26.6 us (23%)
  starting transfers between devices  21.7 us (18%)
  other arithmetic  14.8 us (13%)
  local copies, waits for them, and re-layouts  12.1 us (10%)
  matrix products  5.98 us (5%)
    all_to_all x1, blocking collectives, potential(): lax.all_to_all(scaled_back, 'fft', split_axis=2, concat_axis=3, tiled=True)  26.6 us
    all_to_all x1, waiting for transfers between devices, potential(): lax.all_to_all(along_y, 'fft', split_axis=3, concat_axis=2, tiled=True)  20.6 us
    ppermute x1, waiting for transfers between devices, shifted(): return lax.ppermute(value, axis, pairs)  16.1 us
    all_to_all x1, starting transfers between devices, potential(): lax.all_to_all(along_y, 'fft', split_axis=3, concat_axis=2, tiled=True)  13.5 us
    ppermute x1, starting transfers between devices, shifted(): return lax.ppermute(value, axis, pairs)  8.26 us
    another operation x5, other arithmetic  7.94 us
    dot_general x4, matrix products, apply_table(): return jnp.einsum(form, data, table, preferred_element_type=jnp.float32)  4.06 us
  transfers between devices with their start and end apart: 2, of which 2 were waited for; matrix products, arithmetic and copies ran while one was open for 8% of the time, Pallas kernels for 0%

profile of v1, /device:TPU:1, one launch (start us, length us, event | category | flops | bytes accessed | tf_op | source)
XLA Modules:
  0.0 118.0 jit_solution(2469198560050355938)
XLA Ops:
  0.0 8.3 %collective-permute-start = (bf16[1,2,1,5,25600]{4,1,3,2,0:T(2,128)(2,1)}, bf16[1,2,1,5,25600]{4,1,3,2,0:T(2,128)(2,1)S(1)}, u32[]{:S(2)}, u32[]{:S(2)}) collective-permute-start(bf16[1,2,1,5,25600]{4,1,3,2,0:T(2,128)(2,1)} %param.3), channel_id=1, source_target_pairs={{0,32},{32,64},{64,96},{96,128},{128,160},{160,192},{192,224},{224... | collective-permute-start | bytes 1536008 | tf_op jit(solution)/shard_map/ppermute | solution.py:19
  8.3 0.9 add_select_fusion.2
  9.2 0.9 broadcast_compare_fusion
  10.1 0.8 select_reduce_fusion
  10.9 0.7 fusion.74
  11.6 1.9 %fusion.9 = pred[5,160]{1,0:T(8,128)(4,1)S(1)} fusion(s32[16000]{0:T(1024)S(1)} %get-tuple-element.36, s32[16000]{0:T(1024)S(1)} %get-tuple-element.35, s32[5]{0:T(128)S(1)} %iota_add_fusion, pred[16000]{0:T(1024)(128)(4,1)S(1)} %broadcast_compare_fusion), kind=kOutput, calls=%fused_computation.16 | convolution fusion | flops 28320800 | bytes 144820 | tf_op jit(solution)/shard_map/rs,cs->rc/dot_general | solution.py:118
  14.3 0.7 cosine_convert_fusion
  15.0 0.7 negate_convert_fusion.2
  15.7 16.1 %collective-permute-done = bf16[1,2,1,5,25600]{4,1,3,2,0:T(2,128)(2,1)S(1)} collective-permute-done((bf16[1,2,1,5,25600]{4,1,3,2,0:T(2,128)(2,1)}, bf16[1,2,1,5,25600]{4,1,3,2,0:T(2,128)(2,1)S(1)}, u32[]{:S(2)}, u32[]{:S(2)}) %collective-permute-start) | collective-permute-done | bytes 512032 | tf_op jit(solution)/shard_map/ppermute | solution.py:19
  31.8 4.2 %fusion.35 = (bf16[5,25600]{1,0:T(8,128)(2,1)S(1)}, bf16[5,25600]{1,0:T(8,128)(2,1)S(1)}) fusion(bf16[1,2,1,5,25600]{4,1,3,2,0:T(2,128)(2,1)S(1)} %copy-done, bf16[1,2,1,5,25600]{4,1,3,2,0:T(2,128)(2,1)S(1)} %collective-permute-done), kind=kLoop, calls=%fused_computation.53 | loop fusion | flops 1536000 | bytes 1536000 | tf_op jit(solution)/shard_map/convert.5
  37.1 1.0 fusion.7
  38.1 1.8 %copy.79 = bf16[1,2,5,160,160]{4,1,2,0,3:T(2,128)(2,1)} copy(bf16[1,2,5,160,160]{4,3,2,1,0:T(8,128)(2,1)S(1)} %fusion.7) | data formatting | bytes 1024000 | tf_op jit(solution)/shard_map/while/body/eval_jaxpr/convert_element_type | solution.py:129
  39.9 13.5 %all-to-all-start = ((bf16[1,2,5,160,160]{4,1,2,0,3:T(2,128)(2,1)}), bf16[1,2,5,160,160]{4,1,2,0,3:T(2,128)(2,1)S(1)}, u32[]{:S(2)}, u32[]{:S(2)}) async-start(bf16[1,2,5,160,160]{4,1,2,0,3:T(2,128)(2,1)} %copy.79), calls=%async_computation | async-start | bytes 1638400 | tf_op jit(solution)/shard_map/while/body/eval_jaxpr/all_to_all | solution.py:130
  53.9 1.3 %multiply_add_fusion = f32[800]{0:T(1024)S(1)} fusion(f32[]{:T(128)} %bitcast.30, f32[]{:T(128)} %bitcast.29, pred[800]{0:T(1024)(128)(4,1)S(1)} %gt.21, s32[]{:T(128)S(6)} %mul.330), kind=kLoop, calls=%fused_computation.98 | loop fusion | flops 23200 | bytes 4012 | tf_op jit(solution)/shard_map/add | solution.py:51
  55.8 20.6 %all-to-all-done = bf16[1,2,5,160,160]{4,1,2,0,3:T(2,128)(2,1)S(1)} async-done(((bf16[1,2,5,160,160]{4,1,2,0,3:T(2,128)(2,1)}), bf16[1,2,5,160,160]{4,1,2,0,3:T(2,128)(2,1)S(1)}, u32[]{:S(2)}, u32[]{:S(2)}) %all-to-all-start) | async-done | bytes 512032 | tf_op jit(solution)/shard_map/while/body/eval_jaxpr/all_to_all | solution.py:130
  77.1 1.1 reshape.574
  78.2 1.8 %fusion.4 = bf16[2,160,800]{2,1,0:T(8,128)(2,1)S(1)} fusion(bf16[2,160,800,1]{2,1,0,3:T(8,128)(2,1)S(1)} %reshape.574, f32[160,800]{1,0:T(8,128)S(1)} %fusion.21, bf16[1,160,2,160]{1,3,0,2:T(8,128)(2,1)S(1)} %get-tuple-element.32, bf16[1,160,2,160]{1,3,0,2:T(8,128)(2,1)} %copy-done.1, bf16[1,160,2,160]{1,3,2,0:T(8,128)(2,1)S(1)} %get-tuple-element.34, ...), kind=kOutput, calls=%fused_computation.11 | convolution fusion | flops 328652800 | bytes 1945600 | tf_op jit(solution)/shard_map/while/body/eval_jaxpr/pczs,czdk->pdks/dot_general | solution.py:91
  80.3 1.7 %copy.83 = bf16[1,2,160,5,160]{4,1,3,0,2:T(2,128)(2,1)S(1)} copy(bf16[1,2,160,5,160]{2,4,3,1,0:T(8,128)(2,1)S(1)} %bitcast.188) | data formatting | bytes 1024000 | tf_op jit(solution)/shard_map/while/body/eval_jaxpr/reshape | solution.py:132
  82.0 26.6 %all_to_all.38 = bf16[1,2,160,5,160]{4,1,3,0,2:T(2,128)(2,1)S(1)} all-to-all(bf16[1,2,160,5,160]{4,1,3,0,2:T(2,128)(2,1)S(1)} %copy.83), channel_id=1, replica_groups=mesh['pool'=16,'fft'=32] {'fft'}, dimensions={2} | all-to-all | bytes 1024000 | tf_op jit(solution)/shard_map/while/body/eval_jaxpr/all_to_all | solution.py:133
  110.9 0.9 squeeze.29
  112.3 0.9 squeeze.28
  113.2 1.8 %negate_convert_fusion.1 = (bf16[1,1,1,5,25600]{4,2,3,1,0:T(2,128)(2,1)S(1)}, bf16[1,1,1,5,25600]{4,2,3,1,0:T(2,128)(2,1)S(1)}) fusion(f32[1,1,1,5,25600]{4,2,3,1,0:T(1,128)S(1)} %squeeze.29, f32[1,1,1,5,25600]{4,2,3,1,0:T(1,128)S(1)} %squeeze.28, bf16[1,2,1,5,25600]{4,1,3,2,0:T(2,128)(2,1)S(1)} %collective-permute-done), kind=kLoop, calls=%fused_computation.51 | loop fusion | flops 1536000 | bytes 2048000 | tf_op jit(solution)/shard_map/convert
  115.0 1.7 %pad_maximum_fusion = bf16[1,2,1,5,25600]{4,2,3,1,0:T(2,128)(2,1)S(1)} fusion(bf16[1,1,1,5,25600]{4,2,3,1,0:T(2,128)(2,1)S(1)} %get-tuple-element.30, bf16[1,1,1,5,25600]{4,2,3,1,0:T(2,128)(2,1)S(1)} %get-tuple-element.29), kind=kLoop, calls=%fused_computation.17 | loop fusion | flops 256000 | bytes 1024000 | tf_op jit(solution)/shard_map/stack | solution.py:87
  116.7 1.3 %copy.91 = bf16[1,2,1,5,25600]{4,1,3,2,0:T(2,128)(2,1)} copy(bf16[1,2,1,5,25600]{4,2,3,1,0:T(2,128)(2,1)S(1)} %pad_maximum_fusion) | data formatting | bytes 1024000 | tf_op jit(solution)/shard_map/stack | solution.py:87
  (26 shorter events, 6.8 us)
Async XLA Ops:
  0.0 31.8 %collective-permute-start = (bf16[1,2,1,5,25600]{4,1,3,2,0:T(2,128)(2,1)}, bf16[1,2,1,5,25600]{4,1,3,2,0:T(2,128)(2,1)S(1)}, u32[]{:S(2)}, u32[]{:S(2)}) collective-permute-start(bf16[1,2,1,5,25600]{4,1,3,2,0:T(2,128)(2,1)} %param.3), channel_id=1, source_target_pairs={{0,32},{32,64},{64,96},{96,128},{128,160},{160,192},{192,224},{224... | collective-permute-start | bytes 1536008 | tf_op jit(solution)/shard_map/ppermute | solution.py:19
  11.6 20.2 %copy-start = (bf16[1,2,1,5,25600]{4,1,3,2,0:T(2,128)(2,1)S(1)}, bf16[1,2,1,5,25600]{4,1,3,2,0:T(2,128)(2,1)}, u32[]{:S(2)}) copy-start(bf16[1,2,1,5,25600]{4,1,3,2,0:T(2,128)(2,1)} %param.3) | copy-start | bytes 1536004
  15.7 24.1 %copy-start.1 = (bf16[1,160,2,160]{1,3,0,2:T(8,128)(2,1)}, bf16[1,160,2,160]{1,3,0,2:T(8,128)(2,1)S(1)}, u32[]{:S(2)}) copy-start(bf16[1,160,2,160]{1,3,0,2:T(8,128)(2,1)S(1)} %get-tuple-element.33) | copy-start | bytes 307204
  39.9 36.5 %all-to-all-start = ((bf16[1,2,5,160,160]{4,1,2,0,3:T(2,128)(2,1)}), bf16[1,2,5,160,160]{4,1,2,0,3:T(2,128)(2,1)S(1)}, u32[]{:S(2)}, u32[]{:S(2)}) async-start(bf16[1,2,5,160,160]{4,1,2,0,3:T(2,128)(2,1)} %copy.79), calls=%async_computation | async-start | bytes 1638400 | tf_op jit(solution)/shard_map/while/body/eval_jaxpr/all_to_all | solution.py:130

commit v2 on v0

v2 whole, which is shorter than its diff:
```python
import functools
import math

import jax
import jax.numpy as jnp
import ml_dtypes
import numpy as np
from jax import lax
from jax.experimental import pallas as pl
from jax.experimental.pallas import tpu as pltpu
from jax.sharding import PartitionSpec as P

NG = 160
KMESH = 4
SPACING_BOHR = 0.1875
SCREENING = 0.106

FFT = 32
POOL = 16
PLANES = NG // FFT
ROWS = NG // FFT
QUADS = 4
FOLD = 4
DEEP = NG // FOLD
WIDE = NG * FOLD
BLOCK = (ROWS + 1) * PLANES * 2
PITCH = 72
LANES = 128
STICK_ROWS = 125


def main_kx():
    lanes = np.arange(LANES)
    return np.where(lanes < 64, lanes, lanes + 32)


def edge_kx():
    return 64 + np.arange(LANES) % 32


def edge_ky():
    slots = np.arange(FFT * QUADS)
    return (slots - 64) % NG


def complex_table(inputs, outputs, orientation):
    product = (np.asarray(outputs)[:, None] * np.asarray(inputs)[None, :]) % NG
    angle = product.astype(np.float32) * np.float32(2.0 * math.pi / NG)
    cosine = np.cos(angle)
    sine = orientation * np.sin(angle)
    upper = np.stack([cosine, -sine], axis=1)
    lower = np.stack([sine, cosine], axis=1)
    return np.stack([upper, lower], axis=0).astype(np.float32)


def tables():
    folded = np.arange(NG)
    y_order = 4 * (folded % DEEP) + folded // DEEP
    grid = np.arange(NG)
    ky_main = np.arange(NG).reshape(FFT, ROWS).T.reshape(-1)
    ky_edge = edge_ky().reshape(FFT, QUADS).T.reshape(-1)
    z_order = np.arange(NG).reshape(FFT, PLANES).T.reshape(-1)

    x_main = complex_table(grid, main_kx(), -1.0)
    x_edge = complex_table(grid, edge_kx(), -1.0)
    x_all = np.stack([x_main, x_edge], axis=0)
    fx = x_all.transpose(3, 4, 0, 1, 2).reshape(2 * NG, 4 * LANES)

    def y_table(ky, n):
        full = complex_table(y_order, ky, -1.0)
        return full.reshape(2, n, FFT, 2, NG)

    fym = y_table(ky_main, ROWS).transpose(1, 0, 2, 3, 4).reshape(2 * NG, 2 * NG)
    fye = y_table(ky_edge, QUADS).transpose(0, 2, 1, 3, 4).reshape(2 * FFT, QUADS * 2 * NG)

    fz = complex_table(z_order, grid, -1.0).reshape(2, NG, 2, PLANES, FFT)
    fz = fz.transpose(0, 1, 3, 2, 4).reshape(2 * NG, 2 * NG)
    bz = complex_table(grid, z_order, 1.0).reshape(2, PLANES, FFT, 2, NG)
    bz = bz.transpose(1, 0, 2, 3, 4).reshape(2 * NG, 2 * NG)

    bym = complex_table(ky_main, y_order, 1.0).reshape(2, NG, 2, ROWS, FFT)
    bym = bym.transpose(0, 1, 3, 2, 4).reshape(2 * NG, 2 * NG)
    bye = complex_table(ky_edge, y_order, 1.0).reshape(2, NG, 2, QUADS, FFT)
    bye = bye.transpose(0, 1, 3, 2, 4).reshape(2 * NG, QUADS * 2 * FFT)

    back_main = complex_table(main_kx(), grid, 1.0)
    back_edge = complex_table(edge_kx(), grid, 1.0)
    back = np.stack([back_main, back_edge], axis=0)
    bx = back.transpose(0, 3, 4, 1, 2).reshape(4 * LANES, 2, NG)
    bx = np.pad(bx, ((0, 0), (0, 0), (0, 256 - NG))).reshape(4 * LANES, 512)
    made = (fx, fym, fye, fz, bz, bym, bye, bx)
    return [jnp.asarray(t.astype(ml_dtypes.bfloat16)) for t in made]


def signed(frequency):
    return jnp.where(frequency >= NG // 2, frequency - NG, frequency)


def dot(a, b):
    return jnp.dot(a, b, preferred_element_type=jnp.float32)


def kernel(
    kgrid, orb, stick, fx_h, fym_h, fye_h, fz_h, bz_h, bym_h, bye_h, bx_h,
    out,
    fx, fym, fye, fz, bz, bym, bye, bx,
    wx, wb, rec, t_main, t_edge, acc, weights, mask,
    send1, recv1, send2, recv2,
    table_sem, shift_send, shift_recv, a_send, a_recv, b_send, b_recv,
):
    pool = lax.axis_index("pool")
    me = lax.axis_index("fft")
    after = lax.rem(pool + 1, POOL)
    before = lax.rem(pool + POOL - 1, POOL)
    mesh_id = pl.DeviceIdType.MESH

    barrier = pltpu.get_barrier_semaphore()
    pl.semaphore_signal(barrier, inc=1, device_id=(after, me), device_id_type=mesh_id)
    pl.semaphore_signal(barrier, inc=1, device_id=(before, me), device_id_type=mesh_id)

    def greet(k, carry):
        peer = lax.rem(me + k, FFT)
        pl.semaphore_signal(barrier, inc=1, device_id=(pool, peer), device_id_type=mesh_id)
        return carry

    lax.fori_loop(1, FFT, greet, 0)
    pairs = ((fx_h, fx), (fym_h, fym), (fye_h, fye), (fz_h, fz), (bz_h, bz), (bym_h, bym), (bye_h, bye), (bx_h, bx))
    loads = [pltpu.make_async_copy(far, near, table_sem.at[i]) for i, (far, near) in enumerate(pairs)]
    for load in loads:
        load.start()
    pl.semaphore_wait(barrier, FFT + 1)

    def shift(z):
        return pltpu.make_async_remote_copy(
            src_ref=orb.at[:, z], dst_ref=rec.at[:, z],
            send_sem=shift_send.at[z], recv_sem=shift_recv.at[z],
            device_id=(after, me), device_id_type=mesh_id,
        )

    for z in range(PLANES):
        shift(z).start()

    row8 = lax.broadcasted_iota(jnp.int32, (16, LANES), 0)
    edge_row = me * QUADS + (row8 - 8) - 64
    edge_row = jnp.where(edge_row < 0, edge_row + NG, edge_row)
    own_ky = jnp.where(row8 < ROWS, me * ROWS + row8, jnp.where((row8 >= 8) & (row8 < 8 + QUADS), edge_row, -7))
    rank = lax.broadcasted_iota(jnp.int32, (2 * LANES, LANES), 0)
    kx_main = jnp.where(rank < 64, rank, rank + 32)
    kx_edge = 64 + lax.rem(rank, 32)
    every_kx = jnp.where(rank < LANES, kx_main, kx_edge)

    def count(i, total):
        slots = stick[pl.ds(i, 1), :]
        ky = jnp.where(slots >= 0, slots // NG, -9)
        kx = slots - (slots // NG) * NG
        hit_y = jnp.where(own_ky == ky, 1.0, 0.0).astype(jnp.bfloat16)
        hit_x = jnp.where(every_kx == kx, 1.0, 0.0).astype(jnp.bfloat16)
        return total + lax.dot_general(hit_y, hit_x, (((1,), (1,)), ((), ())), preferred_element_type=jnp.float32)

    mask[...] = lax.fori_loop(0, STICK_ROWS, count, jnp.zeros((16, 2 * LANES), jnp.float32))

    q = [(kgrid[pool, i] - kgrid[before, i]).astype(jnp.float32) / KMESH for i in range(3)]
    lane = lax.broadcasted_iota(jnp.int32, (NG, LANES), 1)
    freq_z = signed(lax.broadcasted_iota(jnp.int32, (NG, LANES), 0))
    wave_z = freq_z.astype(jnp.float32) + q[2]
    cell = SPACING_BOHR * NG
    quad = lax.broadcasted_iota(jnp.int32, (1, LANES), 1) // 32
    for r in range(ROWS + 1):
        if r < ROWS:
            freq_x = jnp.where(lane < 64, lane, lane - LANES)
            freq_y = jnp.full((NG, LANES), signed(me * ROWS + r), jnp.int32)
            held = mask[pl.ds(r, 1), pl.ds(0, LANES)]
        else:
            freq_x = signed(64 + lax.rem(lane, 32))
            freq_y = me * QUADS + lane // 32 - 64
            held = jnp.zeros((1, LANES), jnp.float32)
            for e in range(QUADS):
                held = jnp.where(quad == e, mask[pl.ds(8 + e, 1), pl.ds(LANES, LANES)], held)
        inside = freq_x * freq_x + freq_y * freq_y + freq_z * freq_z <= (NG // 2) * (NG // 2)
        wave_x = freq_x.astype(jnp.float32) + q[0]
        wave_y = freq_y.astype(jnp.float32) + q[1]
        square = wave_z * wave_z + (wave_x * wave_x + wave_y * wave_y)
        exponent = math.pi * math.pi * square / (cell * cell * SCREENING * SCREENING)
        weight = cell * cell / math.pi * (1.0 - jnp.exp(-exponent)) / square / float(NG) ** 3
        weights[r] = jnp.where(inside & (held > 0.5), weight, 0.0)

    for load in loads:
        load.wait()

    wx[...] = jnp.zeros_like(wx)
    row_i = lax.broadcasted_iota(jnp.int32, (256, 256), 0)
    col_i = lax.broadcasted_iota(jnp.int32, (256, 256), 1)
    for b in range(FOLD):
        for p in range(2):
            wx[b, pl.ds(256 * p + 32 * b, NG), :] = fx[pl.ds(NG * p, NG), :]
            move = jnp.where(col_i == row_i + 32 * b, 1.0, 0.0).astype(jnp.bfloat16)
            wb[b, :, pl.ds(256 * p, 256)] = dot(bx[:, pl.ds(256 * p, 256)], move).astype(jnp.bfloat16)

    lane_quad = lax.broadcasted_iota(jnp.int32, (2 * NG, LANES), 1) // 32

    def forward(z, carry):
        shift(z).wait_recv()
        own_re = orb[0, z].astype(jnp.float32)
        own_im = orb[1, z].astype(jnp.float32)
        rec_re = rec[0, z].astype(jnp.float32)
        rec_im = rec[1, z].astype(jnp.float32)
        den_re = (rec_re * own_re + rec_im * own_im).astype(jnp.bfloat16)
        den_im = (rec_re * own_im - rec_im * own_re).astype(jnp.bfloat16)
        for b in range(FOLD):
            window = slice(128 * b, 128 * b + 256)
            along = dot(den_re[:, window], wx[b, :256, :]) + dot(den_im[:, window], wx[b, 256:, :])
            for p in range(2):
                t_main[pl.ds(NG * p + DEEP * b, DEEP), :] = along[:, LANES * p : LANES * (p + 1)]
                t_edge[pl.ds(NG * p + DEEP * b, DEEP), :] = along[:, LANES * (2 + p) : LANES * (3 + p)]
        made = dot(fym[...], t_main[...].astype(jnp.bfloat16))
        side = t_edge[...]
        edge = jnp.zeros((2 * FFT, LANES), jnp.float32)
        for e in range(QUADS):
            part = jnp.where(lane_quad == e, side, 0.0).astype(jnp.bfloat16)
            edge = edge + dot(fye[:, 2 * NG * e : 2 * NG * (e + 1)], part)
        for r in range(ROWS + 1):
            for p in range(2):
                piece = made[(2 * r + p) * FFT : (2 * r + p + 1) * FFT] if r < ROWS else edge[p * FFT : (p + 1) * FFT]
                acc[pl.ds(10 * r + p + 2 * z, FFT, stride=PITCH), :] = piece
        return carry

    lax.fori_loop(0, PLANES, forward, 0)

    def exchange(send, recv, send_sem, recv_sem):
        send[...] = acc[...].reshape(FFT, PITCH, LANES)[:, :BLOCK].astype(jnp.bfloat16)

        def copy(k):
            peer = lax.rem(me + k, FFT)
            return pltpu.make_async_remote_copy(
                src_ref=send.at[peer], dst_ref=recv.at[me],
                send_sem=send_sem.at[peer], recv_sem=recv_sem.at[me],
                device_id=(pool, peer), device_id_type=mesh_id,
            )

        def start(k, carry):
            copy(k).start()
            return carry

        lax.fori_loop(1, FFT, start, 0)
        recv[me] = send[me]

        def finish(k, carry):
            peer = lax.rem(me + k, FFT)
            pltpu.make_async_remote_copy(
                src_ref=send.at[peer], dst_ref=recv.at[peer],
                send_sem=send_sem.at[peer], recv_sem=recv_sem.at[peer],
                device_id=(pool, peer), device_id_type=mesh_id,
            ).wait_recv()
            return carry

        lax.fori_loop(1, FFT, finish, 0)

        def spread(d, carry):
            acc[pl.ds(pl.multiple_of(d * PITCH, 8), BLOCK), :] = recv[d].astype(jnp.float32)
            return carry

        lax.fori_loop(0, FFT, spread, 0)
        return copy

    first = exchange(send1, recv1, a_send, a_recv)

    def columns(start):
        return acc[pl.ds(start, FFT, stride=PITCH), :]

    for r in range(ROWS + 1):
        field = jnp.concatenate([columns(10 * r + i) for i in range(2 * PLANES)], axis=0).astype(jnp.bfloat16)
        spectrum = dot(fz[...], field)
        weight = weights[r]
        scaled = jnp.concatenate([spectrum[:NG] * weight, spectrum[NG:] * weight], axis=0).astype(jnp.bfloat16)
        returned = dot(bz[...], scaled)
        for i in range(2 * PLANES):
            acc[pl.ds(10 * r + i, FFT, stride=PITCH), :] = returned[FFT * i : FFT * (i + 1)]

    second = exchange(send2, recv2, b_send, b_recv)

    def inverse(z, carry):
        main = jnp.concatenate([columns(10 * r + p + 2 * z) for r in range(ROWS) for p in range(2)], axis=0)
        edge = jnp.concatenate([columns(10 * ROWS + p + 2 * z) for p in range(2)], axis=0)
        quads = lane_quad[: 2 * FFT]
        edges = jnp.concatenate([jnp.where(quads == e, edge, 0.0) for e in range(QUADS)], axis=0)
        t_main[...] = dot(bym[...], main.astype(jnp.bfloat16))
        t_edge[...] = dot(bye[...], edges.astype(jnp.bfloat16))
        shares = []
        for b in range(FOLD):
            parts = [t[pl.ds(NG * p + DEEP * b, DEEP), :] for t in (t_main, t_edge) for p in range(2)]
            shares.append(dot(jnp.concatenate(parts, axis=1).astype(jnp.bfloat16), wb[b]))
        rec_re = rec[0, z].astype(jnp.float32)
        rec_im = rec[1, z].astype(jnp.float32)
        field = []
        for p in range(2):
            lo = [s[:, 256 * p : 256 * p + 128] for s in shares]
            hi = [s[:, 256 * p + 128 : 256 * p + 256] for s in shares]
            tiles = [lo[0]] + [hi[b] + lo[b + 1] for b in range(FOLD - 1)] + [hi[FOLD - 1]]
            field.append(jnp.concatenate(tiles, axis=1))
        out[0, z] = (rec_im * field[1] - rec_re * field[0]).astype(jnp.bfloat16)
        out[1, z] = (-(rec_re * field[1] + rec_im * field[0])).astype(jnp.bfloat16)
        return carry

    lax.fori_loop(0, PLANES, inverse, 0)

    for z in range(PLANES):
        shift(z).wait_send()

    def drain(k, carry):
        first(k).wait_send()
        second(k).wait_send()
        return carry

    lax.fori_loop(1, FFT, drain, 0)


def local(orbitals, stick_map, kpoint_grid):
    orb = orbitals.reshape(2, PLANES, DEEP, WIDE)
    stick = stick_map.reshape(STICK_ROWS, LANES)
    constants = tables()
    vmem = pl.BlockSpec(memory_space=pltpu.VMEM)
    anywhere = pl.BlockSpec(memory_space=pl.ANY)
    bf16 = jnp.bfloat16
    result = pl.pallas_call(
        kernel,
        name="exchange_step",
        out_shape=jax.ShapeDtypeStruct(orb.shape, bf16),
        in_specs=[pl.BlockSpec(memory_space=pltpu.SMEM), vmem, vmem] + [anywhere] * len(constants),
        out_specs=vmem,
        scratch_shapes=[pltpu.VMEM(t.shape, bf16) for t in constants]
        + [
            pltpu.VMEM((FOLD, 512, 512), bf16),
            pltpu.VMEM((FOLD, 512, 512), bf16),
            pltpu.VMEM(orb.shape, bf16),
            pltpu.VMEM((2 * NG, LANES), jnp.float32),
            pltpu.VMEM((2 * NG, LANES), jnp.float32),
            pltpu.VMEM((FFT * PITCH, LANES), jnp.float32),
            pltpu.VMEM((ROWS + 1, NG, LANES), jnp.float32),
            pltpu.VMEM((16, 2 * LANES), jnp.float32),
        ]
        + [pltpu.VMEM((FFT, BLOCK, LANES), bf16)] * 4
        + [
            pltpu.SemaphoreType.DMA((len(constants),)),
            pltpu.SemaphoreType.DMA((PLANES,)),
            pltpu.SemaphoreType.DMA((PLANES,)),
        ]
        + [pltpu.SemaphoreType.DMA((FFT,))] * 4,
        compiler_params=pltpu.CompilerParams(
            collective_id=0, has_side_effects=True, vmem_limit_bytes=48 * 1024 * 1024
        ),
    )(kpoint_grid, orb, stick, *constants)
    return result.reshape(1, 2, 1, PLANES, NG * NG)


def solution(mesh):
    return jax.shard_map(
        local,
        mesh=mesh,
        in_specs=(P("pool", None, None, "fft", None), P(), P()),
        out_specs=P("pool", None, None, "fft", None),
        check_vma=False,
    )
```

time: 174 us -> 83.1 us (0.48)
  local copies, waits for them, and re-layouts: 84.9 us -> 6.04 us
  Pallas kernels: 0 us -> 76.7 us
  blocking collectives: 26.6 us -> 0 us
  other arithmetic: 22.1 us -> 0 us
  waiting for transfers between devices: 20.5 us -> 0 us
  starting transfers between devices: 14 us -> 0 us
  matrix products: 4.07 us -> 0 us
    pallas_call x0 -> x1, Pallas kernels: none -> 76.7 us  [local(): pl.pallas_call(kernel, name='exchange_step', out_shape=jax.ShapeDtypeStru...]
    gather x15 -> x0, local copies, waits for them, and re-layouts: 73 us -> none  [the longest x14 68.1 us: local(): found_at = jnp.searchsorted(ordered_map, share_ids)]
    all_to_all x1 -> x0, blocking collectives: 26.6 us -> none  [potential(): lax.all_to_all(scaled_back, 'fft', split_axis=2, concat_axis=3, tiled=True)]
    all_to_all x1 -> x0, waiting for transfers between devices: 20.5 us -> none  [potential(): lax.all_to_all(along_y, 'fft', split_axis=3, concat_axis=2, tiled=True)]
    another operation x7 -> x0, other arithmetic: 9.69 us -> none
    sort x1 -> x0, other arithmetic: 8.6 us -> none  [local(): ordered_map = jnp.sort(stick_map)]
    ppermute x1 -> x0, starting transfers between devices: 8.26 us -> none  [shifted(): return lax.ppermute(value, axis, pairs)]
    all_to_all x1 -> x0, starting transfers between devices: 5.75 us -> none  [potential(): lax.all_to_all(along_y, 'fft', split_axis=3, concat_axis=2, tiled=True)]
  transfers between devices with their start and end apart: 2 -> 0, of which waited for: 1 -> 0; matrix products, arithmetic and copies ran while one was open for 51% -> 0% of each run, Pallas kernels for 0% -> 0%
where the time goes in v2:
time: 83.1 us; the launch traced here: 82.9 us
  Pallas kernels  76.7 us (92%)
  local copies, waits for them, and re-layouts  6.04 us (7%)
    pallas_call x1, Pallas kernels, local(): pl.pallas_call(kernel, name='exchange_step', out_shape=jax.ShapeDtypeStru...  76.7 us
    unnamed x19, local copies, waits for them, and re-layouts  3.58 us

profile of v2, /device:TPU:1, one launch (start us, length us, event | category | flops | bytes accessed | tf_op | source)
XLA Modules:
  0.0 82.9 jit_solution(7364437590728904999)
XLA Ops:
  0.0 0.8 copy.15.kgrid
  0.8 0.0 copy-start.2
  0.8 0.0 copy-start.3
  0.8 0.0 copy-start.4
  0.8 0.0 copy-start.5
  0.8 1.4 %reshape.9 = bf16[2,5,40,640]{3,2,0,1:T(8,128)(2,1)S(1)} reshape(bf16[1,2,1,5,25600]{4,1,3,2,0:T(2,128)(2,1)} %param.11) | data formatting | bytes 1024000 | tf_op jit(solution)/shard_map/reshape | solution.py:318
  2.2 0.0 copy-start
  2.2 0.0 copy-start.1
  2.2 0.0 copy-start.6
  2.3 0.0 copy-done.2
  2.3 0.0 copy-done.3
  2.3 0.0 copy-done.4
  2.3 0.0 copy-done.5
  2.4 0.9 %copy-done = bf16[512,512]{1,0:T(8,128)(2,1)S(1)} copy-done((bf16[512,512]{1,0:T(8,128)(2,1)S(1)}, bf16[512,512]{1,0:T(8,128)(2,1)}, u32[]{:S(2)}) %copy-start) | copy-done | bytes 524312
  3.3 0.1 copy-done.1
  3.4 0.0 copy-done.6
  3.4 0.0 copy-start.7
  3.4 0.9 %copy-done.7 = bf16[64,1280]{1,0:T(8,128)(2,1)S(1)} copy-done((bf16[64,1280]{1,0:T(8,128)(2,1)S(1)}, bf16[64,1280]{1,0:T(8,128)(2,1)}, u32[]{:S(2)}) %copy-start.7) | copy-done | bytes 163864
  4.3 0.0 copy-start.8
  4.3 0.8 %copy-done.8 = s32[16000]{0:T(1024)S(1)} copy-done((s32[16000]{0:T(1024)S(1)}, s32[16000]{0:T(1024)}, u32[]{:S(2)}) %copy-start.8) | copy-done | bytes 64024
  5.2 76.7 %exchange_step.1 = bf16[2,5,40,640]{3,2,1,0:T(8,128)(2,1)S(1)} custom-call(s32[16,3]{1,0:T(8,128)S(1)} %copy.15.kgrid, bf16[2,5,40,640]{3,2,1,0:T(8,128)(2,1)S(1)} %copy.16.orb, s32[125,128]{1,0:T(8,128)S(1)} %bitcast.7, bf16[320,512]{1,0:T(8,128)(2,1)S(1)} %copy-done.1, bf16[320,320]{1,0:T(8,128)(2,1)S(1)} %copy-done.5, bf16[64,1280]{1,0:T(8,128)(2,1)S(1)} %copy-done.7, ...), custom_call_target="tpu_custom_call" | custom-call | tf_op jit(solution)/shard_map/exchange_step/pallas_call | solution.py:324
  82.0 0.9 %reshape.11 = bf16[1,2,1,5,25600]{4,1,3,2,0:T(2,128)(2,1)} reshape(bf16[2,5,40,640]{3,2,0,1:T(8,128)(2,1)S(1)} %copy.17) | data formatting | bytes 1024000 | tf_op jit(solution)/shard_map/reshape | solution.py:352
  (2 shorter events, 0.1 us)
Async XLA Ops:
  0.8 1.6 %copy-start.2 = (bf16[320,320]{1,0:T(8,128)(2,1)S(1)}, bf16[320,320]{1,0:T(8,128)(2,1)}, u32[]{:S(2)}) copy-start(bf16[320,320]{1,0:T(8,128)(2,1)} %constant.21.clone.bym_h) | copy-start | bytes 614404
  0.8 1.6 %copy-start.3 = (bf16[320,320]{1,0:T(8,128)(2,1)S(1)}, bf16[320,320]{1,0:T(8,128)(2,1)}, u32[]{:S(2)}) copy-start(bf16[320,320]{1,0:T(8,128)(2,1)} %constant.20.clone.bz_h) | copy-start | bytes 614404
  0.8 1.6 %copy-start.4 = (bf16[320,320]{1,0:T(8,128)(2,1)S(1)}, bf16[320,320]{1,0:T(8,128)(2,1)}, u32[]{:S(2)}) copy-start(bf16[320,320]{1,0:T(8,128)(2,1)} %constant.19.clone.fz_h) | copy-start | bytes 614404
  0.8 1.6 %copy-start.5 = (bf16[320,320]{1,0:T(8,128)(2,1)S(1)}, bf16[320,320]{1,0:T(8,128)(2,1)}, u32[]{:S(2)}) copy-start(bf16[320,320]{1,0:T(8,128)(2,1)} %constant.17.clone.fym_h) | copy-start | bytes 614404
  2.2 1.0 %copy-start = (bf16[512,512]{1,0:T(8,128)(2,1)S(1)}, bf16[512,512]{1,0:T(8,128)(2,1)}, u32[]{:S(2)}) copy-start(bf16[512,512]{1,0:T(8,128)(2,1)} %constant.23.clone.bx_h) | copy-start | bytes 1572868
  2.2 1.1 %copy-start.1 = (bf16[320,512]{1,0:T(8,128)(2,1)S(1)}, bf16[320,512]{1,0:T(8,128)(2,1)}, u32[]{:S(2)}) copy-start(bf16[320,512]{1,0:T(8,128)(2,1)} %constant.16.clone.fx_h) | copy-start | bytes 983044
  2.2 1.2 %copy-start.6 = (bf16[320,256]{1,0:T(8,128)(2,1)S(1)}, bf16[320,256]{1,0:T(8,128)(2,1)}, u32[]{:S(2)}) copy-start(bf16[320,256]{1,0:T(8,128)(2,1)} %constant.22.clone.bye_h) | copy-start | bytes 491524
  3.4 0.9 %copy-start.7 = (bf16[64,1280]{1,0:T(8,128)(2,1)S(1)}, bf16[64,1280]{1,0:T(8,128)(2,1)}, u32[]{:S(2)}) copy-start(bf16[64,1280]{1,0:T(8,128)(2,1)} %constant.18.clone.fye_h) | copy-start | bytes 491524
  4.3 0.8 %copy-start.8 = (s32[16000]{0:T(1024)S(1)}, s32[16000]{0:T(1024)}, u32[]{:S(2)}) copy-start(s32[16000]{0:T(1024)} %param.12) | copy-start | bytes 192004

commit v3 on v2

v3 whole, which is shorter than its diff:
```python
import functools
import math

import jax
import jax.numpy as jnp
import ml_dtypes
import numpy as np
from jax import lax
from jax.experimental import pallas as pl
from jax.experimental.pallas import tpu as pltpu
from jax.sharding import PartitionSpec as P

NG = 160
KMESH = 4
SPACING_BOHR = 0.1875
SCREENING = 0.106

FFT = 32
POOL = 16
PLANES = NG // FFT
ROWS = NG // FFT
QUADS = 4
FOLD = 4
DEEP = NG // FOLD
WIDE = NG * FOLD
GROUPS = ROWS + 1
PIECE = GROUPS * 2
PITCH = 24
TILES = WIDE // 128
RAW = 2 * TILES * DEEP
OTHERS = FFT - 1
LANES = 128
STICK_ROWS = 125


def main_kx():
    lanes = np.arange(LANES)
    return np.where(lanes < 64, lanes, lanes + 32)


def edge_kx():
    return 64 + np.arange(LANES) % 32


def edge_ky():
    slots = np.arange(FFT * QUADS)
    return (slots - 64) % NG


def complex_table(inputs, outputs, orientation):
    product = (np.asarray(outputs)[:, None] * np.asarray(inputs)[None, :]) % NG
    angle = product.astype(np.float32) * np.float32(2.0 * math.pi / NG)
    cosine = np.cos(angle)
    sine = orientation * np.sin(angle)
    upper = np.stack([cosine, -sine], axis=1)
    lower = np.stack([sine, cosine], axis=1)
    return np.stack([upper, lower], axis=0).astype(np.float32)


def tables():
    folded = np.arange(NG)
    y_order = 4 * (folded % DEEP) + folded // DEEP
    grid = np.arange(NG)
    ky_main = np.arange(NG).reshape(FFT, ROWS).T.reshape(-1)
    ky_edge = edge_ky().reshape(FFT, QUADS).T.reshape(-1)
    z_order = np.arange(NG).reshape(FFT, PLANES).T.reshape(-1)

    x_main = complex_table(grid, main_kx(), -1.0)
    x_edge = complex_table(grid, edge_kx(), -1.0)
    x_all = np.stack([x_main, x_edge], axis=0)
    fx = x_all.transpose(3, 4, 0, 1, 2).reshape(2 * NG, 4 * LANES)

    def y_table(ky, n):
        full = complex_table(y_order, ky, -1.0)
        return full.reshape(2, n, FFT, 2, NG)

    fym = y_table(ky_main, ROWS).transpose(1, 0, 2, 3, 4).reshape(2 * NG, 2 * NG)
    fye = y_table(ky_edge, QUADS).transpose(0, 2, 1, 3, 4).reshape(2 * FFT, QUADS * 2 * NG)

    fz = complex_table(z_order, grid, -1.0).reshape(2, NG, 2, PLANES, FFT)
    fz = fz.transpose(0, 1, 3, 2, 4).reshape(2 * NG, 2 * NG)
    bz = complex_table(grid, z_order, 1.0).reshape(2, PLANES, FFT, 2, NG)
    bz = bz.transpose(1, 0, 2, 3, 4).reshape(2 * NG, 2 * NG)

    bym = complex_table(ky_main, y_order, 1.0).reshape(2, NG, 2, ROWS, FFT)
    bym = bym.transpose(0, 1, 3, 2, 4).reshape(2 * NG, 2 * NG)
    bye = complex_table(ky_edge, y_order, 1.0).reshape(2, NG, 2, QUADS, FFT)
    bye = bye.transpose(0, 1, 3, 2, 4).reshape(2 * NG, QUADS * 2 * FFT)

    back_main = complex_table(main_kx(), grid, 1.0)
    back_edge = complex_table(edge_kx(), grid, 1.0)
    back = np.stack([back_main, back_edge], axis=0)
    bx = back.transpose(0, 3, 4, 1, 2).reshape(4 * LANES, 2, NG)
    bx = np.pad(bx, ((0, 0), (0, 0), (0, 256 - NG))).reshape(4 * LANES, 512)
    made = (fx, fym, fye, fz, bz, bym, bye, bx)
    return [jnp.asarray(t.astype(ml_dtypes.bfloat16)) for t in made]


def signed(frequency):
    return jnp.where(frequency >= NG // 2, frequency - NG, frequency)


def dot(a, b):
    return jnp.dot(a, b, preferred_element_type=jnp.float32)


def kernel(
    kgrid_h, orb, stick_h, fx_h, fym_h, fye_h, fz_h, bz_h, bym_h, bye_h, bx_h,
    out,
    kgrid, own, stick, fx, fym, fye, fz, bz, bym, bye, bx,
    wx, wb, rec, flat_a, flat_b, t_main, t_edge, stage, acc, weights, scaled, mask,
    send1, recv1, send2, recv2,
    load_sem, shift_send, shift_recv, a_send, a_recv, b_send, b_recv,
):
    pool = lax.axis_index("pool")
    me = lax.axis_index("fft")
    after = lax.rem(pool + 1, POOL)
    before = lax.rem(pool + POOL - 1, POOL)
    mesh_id = pl.DeviceIdType.MESH

    barrier = pltpu.get_barrier_semaphore()
    pl.semaphore_signal(barrier, inc=1, device_id=(before, me), device_id_type=mesh_id)

    def greet(k, carry):
        peer = lax.rem(me + k, FFT)
        pl.semaphore_signal(barrier, inc=1, device_id=(pool, peer), device_id_type=mesh_id)
        return carry

    lax.fori_loop(1, FFT, greet, 0)
    pairs = (
        (stick_h, stick), (kgrid_h, kgrid), (orb, own), (fx_h, fx), (bx_h, bx), (fym_h, fym),
        (fye_h, fye), (fz_h, fz), (bz_h, bz), (bym_h, bym), (bye_h, bye),
    )
    loads = [pltpu.make_async_copy(far, near, load_sem.at[i]) for i, (far, near) in enumerate(pairs)]
    for load in loads:
        load.start()
    pl.semaphore_wait(barrier, FFT)

    def shift(z):
        return pltpu.make_async_remote_copy(
            src_ref=orb.at[z], dst_ref=rec.at[z],
            send_sem=shift_send.at[z], recv_sem=shift_recv.at[z],
            device_id=(after, me), device_id_type=mesh_id,
        )

    for z in range(PLANES):
        shift(z).start()
    for load in loads:
        load.wait()

    row16 = lax.broadcasted_iota(jnp.int32, (16, LANES), 0)
    edge_row = me * QUADS + (row16 - 8) - 64
    edge_row = jnp.where(edge_row < 0, edge_row + NG, edge_row)
    own_ky = jnp.where(row16 < ROWS, me * ROWS + row16, jnp.where((row16 >= 8) & (row16 < 8 + QUADS), edge_row, -7))
    rank = lax.broadcasted_iota(jnp.int32, (2 * LANES, LANES), 0)
    kx_main = jnp.where(rank < 64, rank, rank + 32)
    kx_edge = 64 + lax.rem(rank, 32)
    every_kx = jnp.where(rank < LANES, kx_main, kx_edge)

    def count(i, total):
        hits_y, hits_x = [], []
        for u in range(5):
            slots = stick[pl.ds(5 * i + u, 1), :]
            row = slots // NG
            ky = jnp.where(slots >= 0, row, -9)
            kx = slots - row * NG
            hits_y.append(jnp.where(own_ky == ky, 1.0, 0.0))
            hits_x.append(jnp.where(every_kx == kx, 1.0, 0.0))
        hit_y = jnp.concatenate(hits_y, axis=1).astype(jnp.bfloat16)
        hit_x = jnp.concatenate(hits_x, axis=1).astype(jnp.bfloat16)
        return total + lax.dot_general(hit_y, hit_x, (((1,), (1,)), ((), ())), preferred_element_type=jnp.float32)

    mask[...] = lax.fori_loop(0, STICK_ROWS // 5, count, jnp.zeros((16, 2 * LANES), jnp.float32))

    pools = lax.broadcasted_iota(jnp.int32, (3, POOL), 1)
    moved = jnp.where(pools == pool, kgrid[...], 0) - jnp.where(pools == before, kgrid[...], 0)
    q = jnp.sum(moved.astype(jnp.float32), axis=1, keepdims=True) / KMESH
    lane = lax.broadcasted_iota(jnp.int32, (NG, LANES), 1)
    freq_z = signed(lax.broadcasted_iota(jnp.int32, (NG, LANES), 0))
    wave_z = freq_z.astype(jnp.float32) + q[2:3]
    cell = SPACING_BOHR * NG
    quad = lax.broadcasted_iota(jnp.int32, (1, LANES), 1) // 32
    for r in range(GROUPS):
        if r < ROWS:
            freq_x = jnp.where(lane < 64, lane, lane - LANES)
            freq_y = jnp.full((NG, LANES), signed(me * ROWS + r), jnp.int32)
            held = mask[pl.ds(r, 1), pl.ds(0, LANES)]
        else:
            freq_x = signed(64 + lax.rem(lane, 32))
            freq_y = me * QUADS + lane // 32 - 64
            held = jnp.zeros((1, LANES), jnp.float32)
            for e in range(QUADS):
                held = jnp.where(quad == e, mask[pl.ds(8 + e, 1), pl.ds(LANES, LANES)], held)
        inside = freq_x * freq_x + freq_y * freq_y + freq_z * freq_z <= (NG // 2) * (NG // 2)
        wave_x = freq_x.astype(jnp.float32) + q[0:1]
        wave_y = freq_y.astype(jnp.float32) + q[1:2]
        square = wave_z * wave_z + (wave_x * wave_x + wave_y * wave_y)
        exponent = math.pi * math.pi * square / (cell * cell * SCREENING * SCREENING)
        weight = cell * cell / math.pi * (1.0 - jnp.exp(-exponent)) / square / float(NG) ** 3
        weights[:, pl.ds(LANES * r, LANES)] = jnp.where(inside & (held > 0.5), weight, 0.0)

    wx[...] = jnp.zeros_like(wx)
    row_i = lax.broadcasted_iota(jnp.int32, (256, 256), 0)
    col_i = lax.broadcasted_iota(jnp.int32, (256, 256), 1)
    for b in range(FOLD):
        move = jnp.where(col_i == row_i + 32 * b, 1.0, 0.0).astype(jnp.bfloat16)
        for p in range(2):
            wx[b, pl.ds(256 * p + 32 * b, NG), :] = fx[pl.ds(NG * p, NG), :]
            wb[b, :, pl.ds(256 * p, 256)] = dot(bx[:, pl.ds(256 * p, 256)], move).astype(jnp.bfloat16)

    lane_quad = lax.broadcasted_iota(jnp.int32, (2 * NG, LANES), 1) // 32

    def piece_to(z, peer, send, recv, send_sem, recv_sem):
        return pltpu.make_async_remote_copy(
            src_ref=send.at[z, peer], dst_ref=recv.at[z, me],
            send_sem=send_sem, recv_sem=recv_sem,
            device_id=(pool, peer), device_id_type=mesh_id,
        )

    def post(z, send, recv, send_sem, recv_sem):
        send[z] = stage[...].reshape(FFT, PITCH, LANES)[:, :PIECE].astype(jnp.bfloat16)
        recv[z, me] = send[z, me]

        def start(k, carry):
            piece_to(z, lax.rem(me + k, FFT), send, recv, send_sem, recv_sem).start()
            return carry

        lax.fori_loop(1, FFT, start, 0)

    def halves(source, t):
        return [source[pl.ds(2 * t + p, DEEP, stride=2 * TILES), :] for p in range(2)]

    def forward(z, carry):
        flat_a[...] = own[z].astype(jnp.float32)
        shift(z).wait_recv()
        flat_b[...] = rec[z].astype(jnp.float32)
        den_re, den_im = [], []
        for t in range(TILES):
            own_re, own_im = halves(flat_a, t)
            rec_re, rec_im = halves(flat_b, t)
            den_re.append((rec_re * own_re + rec_im * own_im).astype(jnp.bfloat16))
            den_im.append((rec_re * own_im - rec_im * own_re).astype(jnp.bfloat16))
        for b in range(FOLD):
            cells = jnp.concatenate(den_re[b : b + 2] + den_im[b : b + 2], axis=1)
            along = dot(cells, wx[b])
            for p in range(2):
                t_main[pl.ds(NG * p + DEEP * b, DEEP), :] = along[:, LANES * p : LANES * (p + 1)]
                t_edge[pl.ds(NG * p + DEEP * b, DEEP), :] = along[:, LANES * (2 + p) : LANES * (3 + p)]
        made = dot(fym[...], t_main[...].astype(jnp.bfloat16))
        side = t_edge[...]
        quads = [jnp.where(lane_quad == e, side, 0.0).astype(jnp.bfloat16) for e in range(QUADS)]
        edge = dot(fye[...], jnp.concatenate(quads, axis=0))
        for r in range(GROUPS):
            for p in range(2):
                piece = made[(2 * r + p) * FFT : (2 * r + p + 1) * FFT] if r < ROWS else edge[p * FFT : (p + 1) * FFT]
                stage[pl.ds(2 * r + p, FFT, stride=PITCH), :] = piece
        post(z, send1, recv1, a_send, a_recv)
        return carry

    lax.fori_loop(0, PLANES, forward, 0)

    everything = (slice(None), pl.ds(0, OTHERS))
    pltpu.make_async_remote_copy(
        src_ref=send1.at[everything], dst_ref=recv1.at[everything], send_sem=a_send, recv_sem=a_recv,
        device_id=(after, me), device_id_type=mesh_id,
    ).wait_recv()

    def spread(d, carry):
        for z in range(PLANES):
            acc[pl.ds(pl.multiple_of((z * FFT + d) * PITCH, 8), PIECE), :] = recv1[z, d].astype(jnp.float32)
        return carry

    lax.fori_loop(0, FFT, spread, 0)
    for r in range(GROUPS):
        runs = [acc[pl.ds(z * FFT * PITCH + 2 * r + p, FFT, stride=PITCH), :] for z in range(PLANES) for p in range(2)]
        spectrum = dot(fz[...], jnp.concatenate(runs, axis=0).astype(jnp.bfloat16))
        weight = weights[:, pl.ds(LANES * r, LANES)]
        for p in range(2):
            scaled[pl.ds(NG * p, NG), pl.ds(LANES * r, LANES)] = (spectrum[NG * p : NG * (p + 1)] * weight).astype(jnp.bfloat16)

    def give_back(z, carry):
        returned = dot(bz[pl.ds(pl.multiple_of(z * 2 * FFT, 2 * FFT), 2 * FFT), :], scaled[...])
        for r in range(GROUPS):
            for p in range(2):
                piece = returned[p * FFT : (p + 1) * FFT, LANES * r : LANES * (r + 1)]
                stage[pl.ds(2 * r + p, FFT, stride=PITCH), :] = piece
        post(z, send2, recv2, b_send, b_recv.at[z])
        return carry

    lax.fori_loop(0, PLANES, give_back, 0)

    def inverse(z, carry):
        flat_b[...] = rec[z].astype(jnp.float32)
        pltpu.make_async_remote_copy(
            src_ref=send2.at[z, pl.ds(0, OTHERS)], dst_ref=recv2.at[z, pl.ds(0, OTHERS)],
            send_sem=b_send, recv_sem=b_recv.at[z],
            device_id=(after, me), device_id_type=mesh_id,
        ).wait_recv()

        def scatter(d, inner):
            stage[pl.ds(pl.multiple_of(d * PITCH, 8), PIECE), :] = recv2[z, d].astype(jnp.float32)
            return inner

        lax.fori_loop(0, FFT, scatter, 0, unroll=8)
        runs = [stage[pl.ds(i, FFT, stride=PITCH), :] for i in range(PIECE)]
        main = jnp.concatenate(runs[: 2 * ROWS], axis=0)
        edge = jnp.concatenate(runs[2 * ROWS :], axis=0)
        quads = lane_quad[: 2 * FFT]
        edges = jnp.concatenate([jnp.where(quads == e, edge, 0.0) for e in range(QUADS)], axis=0)
        t_main[...] = dot(bym[...], main.astype(jnp.bfloat16))
        t_edge[...] = dot(bye[...], edges.astype(jnp.bfloat16))
        shares = []
        for b in range(FOLD):
            parts = [t[pl.ds(NG * p + DEEP * b, DEEP), :] for t in (t_main, t_edge) for p in range(2)]
            shares.append(dot(jnp.concatenate(parts, axis=1).astype(jnp.bfloat16), wb[b]))
        for t in range(TILES):
            field = []
            for p in range(2):
                low, high = 256 * p, 256 * p + 128
                if t == 0:
                    field.append(shares[0][:, low:high])
                elif t == FOLD:
                    field.append(shares[FOLD - 1][:, high : high + 128])
                else:
                    field.append(shares[t - 1][:, high : high + 128] + shares[t][:, low:high])
            rec_re, rec_im = halves(flat_b, t)
            flat_a[pl.ds(2 * t, DEEP, stride=2 * TILES), :] = rec_im * field[1] - rec_re * field[0]
            flat_a[pl.ds(2 * t + 1, DEEP, stride=2 * TILES), :] = -(rec_re * field[1] + rec_im * field[0])
        out[z] = flat_a[...].astype(jnp.bfloat16)
        return carry

    lax.fori_loop(0, PLANES, inverse, 0)

    for z in range(PLANES):
        shift(z).wait_send()
    for send, recv, send_sem, recv_sem in ((send1, recv1, a_send, a_recv), (send2, recv2, b_send, b_recv.at[0])):
        pltpu.make_async_remote_copy(
            src_ref=send.at[everything], dst_ref=recv.at[everything], send_sem=send_sem, recv_sem=recv_sem,
            device_id=(after, me), device_id_type=mesh_id,
        ).wait_send()


def local(orbitals, stick_map, kpoint_grid):
    orb = orbitals.reshape(2, PLANES, TILES * DEEP, LANES).transpose(1, 2, 0, 3).reshape(PLANES, RAW, LANES)
    stick = stick_map.reshape(STICK_ROWS, LANES)
    constants = tables()
    orb, stick, kgrid_t = (pltpu.with_memory_space_constraint(a, pltpu.HBM) for a in (orb, stick, kpoint_grid.T))
    constants = [pltpu.with_memory_space_constraint(c, pltpu.HBM) for c in constants]
    far = pl.BlockSpec(memory_space=pltpu.HBM)
    bf16, f32 = jnp.bfloat16, jnp.float32
    result = pl.pallas_call(
        kernel,
        name="exchange_step",
        out_shape=jax.ShapeDtypeStruct(orb.shape, bf16),
        in_specs=[far] * (3 + len(constants)),
        out_specs=pl.BlockSpec(memory_space=pltpu.VMEM),
        scratch_shapes=[
            pltpu.VMEM((3, POOL), jnp.int32),
            pltpu.VMEM(orb.shape, bf16),
            pltpu.VMEM(stick.shape, jnp.int32),
        ]
        + [pltpu.VMEM(t.shape, bf16) for t in constants]
        + [
            pltpu.VMEM((FOLD, 512, 512), bf16),
            pltpu.VMEM((FOLD, 512, 512), bf16),
            pltpu.VMEM(orb.shape, bf16),
            pltpu.VMEM((RAW, LANES), f32),
            pltpu.VMEM((RAW, LANES), f32),
            pltpu.VMEM((2 * NG, LANES), f32),
            pltpu.VMEM((2 * NG, LANES), f32),
            pltpu.VMEM((FFT * PITCH, LANES), f32),
            pltpu.VMEM((PLANES * FFT * PITCH, LANES), f32),
            pltpu.VMEM((NG, GROUPS * LANES), f32),
            pltpu.VMEM((2 * NG, GROUPS * LANES), bf16),
            pltpu.VMEM((16, 2 * LANES), f32),
        ]
        + [pltpu.VMEM((PLANES, FFT, PIECE, LANES), bf16)] * 4
        + [
            pltpu.SemaphoreType.DMA((3 + len(constants),)),
            pltpu.SemaphoreType.DMA((PLANES,)),
            pltpu.SemaphoreType.DMA((PLANES,)),
            pltpu.SemaphoreType.DMA,
            pltpu.SemaphoreType.DMA,
            pltpu.SemaphoreType.DMA,
            pltpu.SemaphoreType.DMA((PLANES,)),
        ],
        compiler_params=pltpu.CompilerParams(
            collective_id=0, has_side_effects=True, vmem_limit_bytes=48 * 1024 * 1024
        ),
    )(kgrid_t, orb, stick, *constants)
    result = result.reshape(PLANES, TILES * DEEP, 2, LANES).transpose(2, 0, 1, 3)
    return result.reshape(1, 2, 1, PLANES, NG * NG)


def solution(mesh):
    return jax.shard_map(
        local,
        mesh=mesh,
        in_specs=(P("pool", None, None, "fft", None), P(), P()),
        out_specs=P("pool", None, None, "fft", None),
        check_vma=False,
    )
```

time: 83.1 us -> 70.3 us (0.85)
  Pallas kernels: 76.7 us -> 69.4 us
  local copies, waits for them, and re-layouts: 6.04 us -> 0.79 us
    pallas_call x1, Pallas kernels: 76.7 us -> 69.4 us  [local(): pl.pallas_call(kernel, name='exchange_step', out_shape=jax.ShapeDtypeStru...]
    unnamed x19 -> x1, local copies, waits for them, and re-layouts: 3.58 us -> 0.79 us
    reshape x3 -> x0, local copies, waits for them, and re-layouts: 2.41 us -> none  [the longest x2 1.49 us: local(): orb = orbitals.reshape(2, PLANES, DEEP, WIDE)]
where the time goes in v3:
time: 70.3 us; the launch traced here: 70.2 us
  Pallas kernels  69.4 us (99%)
  local copies, waits for them, and re-layouts  0.79 us (1%)
    pallas_call x1, Pallas kernels, local(): pl.pallas_call(kernel, name='exchange_step', out_shape=jax.ShapeDtypeStru...  69.4 us

profile of v3, /device:TPU:1, one launch (start us, length us, event | category | flops | bytes accessed | tf_op | source)
XLA Modules:
  0.0 70.2 jit_solution(13047332077902340359)
XLA Ops:
  0.0 69.4 %exchange_step.1 = bf16[5,400,128]{2,1,0:T(8,128)(2,1)S(1)} custom-call(s32[3,16]{1,0:T(4,128)} %bitcast.15, bf16[5,400,128]{2,1,0:T(8,128)(2,1)} %bitcast.13, s32[125,128]{1,0:T(8,128)} %bitcast.14, bf16[320,512]{1,0:T(8,128)(2,1)} %constant.16.clone.fx_h, bf16[320,320]{1,0:T(8,128)(2,1)} %constant.17.clone.fym_h, bf16[64,1280]{1,0:T(8,128)(2,1)} %constant.18.clone.fye_h, ...), custom_call_target="tpu_custom_call" | custom-call | tf_op jit(solution)/shard_map/exchange_step/pallas_call | solution.py:351
  69.4 0.8 %copy.15 = bf16[1,2,1,5,25600]{4,1,3,2,0:T(2,128)(2,1)} copy(bf16[1,2,1,5,25600]{4,1,3,2,0:T(2,128)(2,1)S(1)} %bitcast.12) | data formatting | bytes 1024000

commit v4 on v3

--- a/solution.py
+++ b/solution.py
@@ -25,7 +25,9 @@
 WIDE = NG * FOLD
 GROUPS = ROWS + 1
 PIECE = GROUPS * 2
-PITCH = 24
+PITCH = 72
+STEPS = ((0, 3), (3, 2))
+OFFSETS = (0, 40)
 TILES = WIDE // 128
 RAW = 2 * TILES * DEEP
 OTHERS = FFT - 1
@@ -108,8 +110,8 @@
     kgrid_h, orb, stick_h, fx_h, fym_h, fye_h, fz_h, bz_h, bym_h, bye_h, bx_h,
     out,
     kgrid, own, stick, fx, fym, fye, fz, bz, bym, bye, bx,
-    wx, wb, rec, flat_a, flat_b, t_main, t_edge, stage, acc, weights, scaled, mask,
-    send1, recv1, send2, recv2,
+    wx, wb, rec, flat_a, flat_b, t_main, t_edge, stage, weights, scaled, mask,
+    send1, recv1, send2, recv2, later1, got1, later2, got2,
     load_sem, shift_send, shift_recv, a_send, a_recv, b_send, b_recv,
 ):
     pool = lax.axis_index("pool")
@@ -210,22 +212,46 @@
 
     lane_quad = lax.broadcasted_iota(jnp.int32, (2 * NG, LANES), 1) // 32
 
-    def piece_to(z, peer, send, recv, send_sem, recv_sem):
+    def row_of(z):
+        return 2 * GROUPS * z + 4 * (z // 3)
+
+    def block_to(peer, send, recv, send_sem, recv_sem):
         return pltpu.make_async_remote_copy(
-            src_ref=send.at[z, peer], dst_ref=recv.at[z, me],
+            src_ref=send.at[peer], dst_ref=recv.at[me],
             send_sem=send_sem, recv_sem=recv_sem,
             device_id=(pool, peer), device_id_type=mesh_id,
         )
 
-    def post(z, send, recv, send_sem, recv_sem):
-        send[z] = stage[...].reshape(FFT, PITCH, LANES)[:, :PIECE].astype(jnp.bfloat16)
-        recv[z, me] = send[z, me]
+    def post(step, send, recv, send_sem, recv_sem):
+        rows = slice(OFFSETS[step], OFFSETS[step] + PIECE * STEPS[step][1])
+        send[...] = stage[...].reshape(FFT, PITCH, LANES)[:, rows].astype(jnp.bfloat16)
 
         def start(k, carry):
-            piece_to(z, lax.rem(me + k, FFT), send, recv, send_sem, recv_sem).start()
+            block_to(lax.rem(me + k, FFT), send, recv, send_sem, recv_sem).start()
             return carry
 
         lax.fori_loop(1, FFT, start, 0)
+        recv[me] = send[me]
+
+    def others(send, recv, send_sem, recv_sem):
+        part = pl.ds(0, OTHERS)
+        return pltpu.make_async_remote_copy(
+            src_ref=send.at[part], dst_ref=recv.at[part], send_sem=send_sem, recv_sem=recv_sem,
+            device_id=(after, me), device_id_type=mesh_id,
+        )
+
+    def collect(step, send, recv, send_sem, recv_sem):
+        others(send, recv, send_sem, recv_sem).wait_recv()
+
+        def spread(d, carry):
+            start = pl.multiple_of(d * PITCH + OFFSETS[step], 8)
+            stage[pl.ds(start, PIECE * STEPS[step][1]), :] = recv[d].astype(jnp.float32)
+            return carry
+
+        lax.fori_loop(0, FFT, spread, 0, unroll=4)
+
+    out_legs = ((send1, recv1, a_send.at[0], a_recv.at[0]), (later1, got1, a_send.at[1], a_recv.at[1]))
+    back_legs = ((send2, recv2, b_send.at[0], b_recv.at[0]), (later2, got2, b_send.at[1], b_recv.at[1]))
 
     def halves(source, t):
         return [source[pl.ds(2 * t + p, DEEP, stride=2 * TILES), :] for p in range(2)]
@@ -253,26 +279,17 @@
         for r in range(GROUPS):
             for p in range(2):
                 piece = made[(2 * r + p) * FFT : (2 * r + p + 1) * FFT] if r < ROWS else edge[p * FFT : (p + 1) * FFT]
-                stage[pl.ds(2 * r + p, FFT, stride=PITCH), :] = piece
-        post(z, send1, recv1, a_send, a_recv)
+                stage[pl.ds(row_of(z) + 2 * r + p, FFT, stride=PITCH), :] = piece
         return carry
 
-    lax.fori_loop(0, PLANES, forward, 0)
-
-    everything = (slice(None), pl.ds(0, OTHERS))
-    pltpu.make_async_remote_copy(
-        src_ref=send1.at[everything], dst_ref=recv1.at[everything], send_sem=a_send, recv_sem=a_recv,
-        device_id=(after, me), device_id_type=mesh_id,
-    ).wait_recv()
-
-    def spread(d, carry):
-        for z in range(PLANES):
-            acc[pl.ds(pl.multiple_of((z * FFT + d) * PITCH, 8), PIECE), :] = recv1[z, d].astype(jnp.float32)
-        return carry
-
-    lax.fori_loop(0, FFT, spread, 0)
+    for step, (first, count_z) in enumerate(STEPS):
+        lax.fori_loop(first, first + count_z, forward, 0)
+        post(step, *out_legs[step])
+
+    for step in range(2):
+        collect(step, *out_legs[step])
     for r in range(GROUPS):
-        runs = [acc[pl.ds(z * FFT * PITCH + 2 * r + p, FFT, stride=PITCH), :] for z in range(PLANES) for p in range(2)]
+        runs = [stage[pl.ds(row_of(z) + 2 * r + p, FFT, stride=PITCH), :] for z in range(PLANES) for p in range(2)]
         spectrum = dot(fz[...], jnp.concatenate(runs, axis=0).astype(jnp.bfloat16))
         weight = weights[:, pl.ds(LANES * r, LANES)]
         for p in range(2):
@@ -283,26 +300,17 @@
         for r in range(GROUPS):
             for p in range(2):
                 piece = returned[p * FFT : (p + 1) * FFT, LANES * r : LANES * (r + 1)]
-                stage[pl.ds(2 * r + p, FFT, stride=PITCH), :] = piece
-        post(z, send2, recv2, b_send, b_recv.at[z])
+                stage[pl.ds(row_of(z) + 2 * r + p, FFT, stride=PITCH), :] = piece
         return carry
 
-    lax.fori_loop(0, PLANES, give_back, 0)
+    for step, (first, count_z) in enumerate(STEPS):
+        lax.fori_loop(first, first + count_z, give_back, 0)
+        post(step, *back_legs[step])
 
     def inverse(z, carry):
         flat_b[...] = rec[z].astype(jnp.float32)
-        pltpu.make_async_remote_copy(
-            src_ref=send2.at[z, pl.ds(0, OTHERS)], dst_ref=recv2.at[z, pl.ds(0, OTHERS)],
-            send_sem=b_send, recv_sem=b_recv.at[z],
-            device_id=(after, me), device_id_type=mesh_id,
-        ).wait_recv()
-
-        def scatter(d, inner):
-            stage[pl.ds(pl.multiple_of(d * PITCH, 8), PIECE), :] = recv2[z, d].astype(jnp.float32)
-            return inner
-
-        lax.fori_loop(0, FFT, scatter, 0, unroll=8)
-        runs = [stage[pl.ds(i, FFT, stride=PITCH), :] for i in range(PIECE)]
+        base = row_of(z)
+        runs = [stage[pl.ds(base + i, FFT, stride=PITCH), :] for i in range(PIECE)]
         main = jnp.concatenate(runs[: 2 * ROWS], axis=0)
         edge = jnp.concatenate(runs[2 * ROWS :], axis=0)
         quads = lane_quad[: 2 * FFT]
@@ -329,15 +337,14 @@
         out[z] = flat_a[...].astype(jnp.bfloat16)
         return carry
 
-    lax.fori_loop(0, PLANES, inverse, 0)
+    for step, (first, count_z) in enumerate(STEPS):
+        collect(step, *back_legs[step])
+        lax.fori_loop(first, first + count_z, inverse, 0)
 
     for z in range(PLANES):
         shift(z).wait_send()
-    for send, recv, send_sem, recv_sem in ((send1, recv1, a_send, a_recv), (send2, recv2, b_send, b_recv.at[0])):
-        pltpu.make_async_remote_copy(
-            src_ref=send.at[everything], dst_ref=recv.at[everything], send_sem=send_sem, recv_sem=recv_sem,
-            device_id=(after, me), device_id_type=mesh_id,
-        ).wait_send()
+    for leg in out_legs + back_legs:
+        others(*leg).wait_send()
 
 
 def local(orbitals, stick_map, kpoint_grid):
@@ -369,21 +376,17 @@
             pltpu.VMEM((2 * NG, LANES), f32),
             pltpu.VMEM((2 * NG, LANES), f32),
             pltpu.VMEM((FFT * PITCH, LANES), f32),
-            pltpu.VMEM((PLANES * FFT * PITCH, LANES), f32),
             pltpu.VMEM((NG, GROUPS * LANES), f32),
             pltpu.VMEM((2 * NG, GROUPS * LANES), bf16),
             pltpu.VMEM((16, 2 * LANES), f32),
         ]
-        + [pltpu.VMEM((PLANES, FFT, PIECE, LANES), bf16)] * 4
+        + [pltpu.VMEM((FFT, PIECE * n, LANES), bf16) for _, n in STEPS for _ in range(4)]
         + [
             pltpu.SemaphoreType.DMA((3 + len(constants),)),
             pltpu.SemaphoreType.DMA((PLANES,)),
             pltpu.SemaphoreType.DMA((PLANES,)),
-            pltpu.SemaphoreType.DMA,
-            pltpu.SemaphoreType.DMA,
-            pltpu.SemaphoreType.DMA,
-            pltpu.SemaphoreType.DMA((PLANES,)),
-        ],
+        ]
+        + [pltpu.SemaphoreType.DMA((2,))] * 4,
         compiler_params=pltpu.CompilerParams(
             collective_id=0, has_side_effects=True, vmem_limit_bytes=48 * 1024 * 1024
         ),

time: 70.3 us -> 66.9 us (0.952)
  Pallas kernels: 69.4 us -> 66 us
    pallas_call x1, Pallas kernels: 69.4 us -> 66 us  [local(): pl.pallas_call(kernel, name='exchange_step', out_shape=jax.ShapeDtypeStru...]
where the time goes in v4:
time: 66.9 us; the launch traced here: 66.8 us
  Pallas kernels  66 us (99%)
  local copies, waits for them, and re-layouts  0.79 us (1%)
    pallas_call x1, Pallas kernels, local(): pl.pallas_call(kernel, name='exchange_step', out_shape=jax.ShapeDtypeStru...  66 us

profile of v4, /device:TPU:1, one launch (start us, length us, event | category | flops | bytes accessed | tf_op | source)
XLA Modules:
  0.0 66.8 jit_solution(482803065286142043)
XLA Ops:
  0.0 66.0 %exchange_step.1 = bf16[5,400,128]{2,1,0:T(8,128)(2,1)S(1)} custom-call(s32[3,16]{1,0:T(4,128)} %bitcast.15, bf16[5,400,128]{2,1,0:T(8,128)(2,1)} %bitcast.13, s32[125,128]{1,0:T(8,128)} %bitcast.14, bf16[320,512]{1,0:T(8,128)(2,1)} %constant.16.clone.fx_h, bf16[320,320]{1,0:T(8,128)(2,1)} %constant.17.clone.fym_h, bf16[64,1280]{1,0:T(8,128)(2,1)} %constant.18.clone.fye_h, ...), custom_call_target="tpu_custom_call" | custom-call | tf_op jit(solution)/shard_map/exchange_step/pallas_call | solution.py:358
  66.0 0.8 %copy.15 = bf16[1,2,1,5,25600]{4,1,3,2,0:T(2,128)(2,1)} copy(bf16[1,2,1,5,25600]{4,1,3,2,0:T(2,128)(2,1)S(1)} %bitcast.12) | data formatting | bytes 1024000

commit v5 on v4

--- a/solution.py
+++ b/solution.py
@@ -20,14 +20,17 @@
 PLANES = NG // FFT
 ROWS = NG // FFT
 QUADS = 4
+EDGE_SHIFT = (-48, -16, 31, 15)
 FOLD = 4
 DEEP = NG // FOLD
 WIDE = NG * FOLD
 GROUPS = ROWS + 1
-PIECE = GROUPS * 2
 PITCH = 72
-STEPS = ((0, 3), (3, 2))
-OFFSETS = (0, 40)
+OUT_ROWS = ((0, 32), (32, 24))
+BACK_ROWS = ((0, 40), (40, 16))
+SHARE = 2 * ROWS + 1
+HALF = 64
+LATE = 14
 TILES = WIDE // 128
 RAW = 2 * TILES * DEEP
 OTHERS = FFT - 1
@@ -35,18 +38,27 @@
 STICK_ROWS = 125
 
 
+def kx_of(quad, place):
+    return np.where(place < 16, 16 * quad + place, place - 32 - 16 * quad)
+
+
 def main_kx():
     lanes = np.arange(LANES)
-    return np.where(lanes < 64, lanes, lanes + 32)
+    return kx_of(lanes // 32, lanes % 32)
 
 
 def edge_kx():
-    return 64 + np.arange(LANES) % 32
+    return kx_of(QUADS, np.arange(LANES) % 32)
+
+
+def main_ky():
+    near = np.arange((ROWS - 1) * FFT).reshape(FFT, ROWS - 1).T
+    near = np.where(near < 64, near, near + 32)
+    return np.concatenate([near, 64 + np.arange(FFT)[None]], axis=0).reshape(-1)
 
 
 def edge_ky():
-    slots = np.arange(FFT * QUADS)
-    return (slots - 64) % NG
+    return (np.array(EDGE_SHIFT)[:, None] + np.arange(FFT)[None]).reshape(-1)
 
 
 def complex_table(inputs, outputs, orientation):
@@ -63,8 +75,8 @@
     folded = np.arange(NG)
     y_order = 4 * (folded % DEEP) + folded // DEEP
     grid = np.arange(NG)
-    ky_main = np.arange(NG).reshape(FFT, ROWS).T.reshape(-1)
-    ky_edge = edge_ky().reshape(FFT, QUADS).T.reshape(-1)
+    ky_main = main_ky()
+    ky_edge = edge_ky()
     z_order = np.arange(NG).reshape(FFT, PLANES).T.reshape(-1)
 
     x_main = complex_table(grid, main_kx(), -1.0)
@@ -102,6 +114,19 @@
     return jnp.where(frequency >= NG // 2, frequency - NG, frequency)
 
 
+def signed_kx(quad, place):
+    return jnp.where(place < 16, 16 * quad + place, place - 32 - 16 * quad)
+
+
+def edge_shift(quad):
+    shift = jnp.where(quad == 0, EDGE_SHIFT[0], EDGE_SHIFT[1])
+    return jnp.where(quad == 2, EDGE_SHIFT[2], jnp.where(quad == 3, EDGE_SHIFT[3], shift))
+
+
+def lent(device, quad):
+    return ((quad == 3) & (device >= 1)) | ((quad == 2) & ((device == 16) | (device == 17)))
+
+
 def dot(a, b):
     return jnp.dot(a, b, preferred_element_type=jnp.float32)
 
@@ -110,7 +135,7 @@
     kgrid_h, orb, stick_h, fx_h, fym_h, fye_h, fz_h, bz_h, bym_h, bye_h, bx_h,
     out,
     kgrid, own, stick, fx, fym, fye, fz, bz, bym, bye, bx,
-    wx, wb, rec, flat_a, flat_b, t_main, t_edge, stage, weights, scaled, mask,
+    wx, rec, flat_a, flat_b, stage, weights, mask,
     send1, recv1, send2, recv2, later1, got1, later2, got2,
     load_sem, shift_send, shift_recv, a_send, a_recv, b_send, b_recv,
 ):
@@ -151,13 +176,15 @@
         load.wait()
 
     row16 = lax.broadcasted_iota(jnp.int32, (16, LANES), 0)
-    edge_row = me * QUADS + (row16 - 8) - 64
+    near_row = me * (ROWS - 1) + row16
+    near_row = jnp.where(near_row < 64, near_row, near_row + 32)
+    near_row = jnp.where(row16 < ROWS - 1, near_row, 64 + me)
+    edge_row = me + edge_shift(row16 - 8)
     edge_row = jnp.where(edge_row < 0, edge_row + NG, edge_row)
-    own_ky = jnp.where(row16 < ROWS, me * ROWS + row16, jnp.where((row16 >= 8) & (row16 < 8 + QUADS), edge_row, -7))
+    own_ky = jnp.where(row16 < ROWS, near_row, jnp.where((row16 >= 8) & (row16 < 8 + QUADS), edge_row, -7))
     rank = lax.broadcasted_iota(jnp.int32, (2 * LANES, LANES), 0)
-    kx_main = jnp.where(rank < 64, rank, rank + 32)
-    kx_edge = 64 + lax.rem(rank, 32)
-    every_kx = jnp.where(rank < LANES, kx_main, kx_edge)
+    every_kx = signed_kx(jnp.where(rank < LANES, rank // 32, QUADS), lax.rem(rank, 32))
+    every_kx = jnp.where(every_kx < 0, every_kx + NG, every_kx)
 
     def count(i, total):
         hits_y, hits_x = [], []
@@ -182,17 +209,24 @@
     wave_z = freq_z.astype(jnp.float32) + q[2:3]
     cell = SPACING_BOHR * NG
     quad = lax.broadcasted_iota(jnp.int32, (1, LANES), 1) // 32
+    outer_held = jnp.zeros((1, LANES), jnp.float32)
+    for e in range(QUADS):
+        outer_held = jnp.where(quad == e, mask[pl.ds(8 + e, 1), pl.ds(LANES, LANES)], outer_held)
+    outer_x = signed_kx(QUADS, lax.rem(lane, 32))
+    outer_y = me + edge_shift(lane // 32)
     for r in range(GROUPS):
-        if r < ROWS:
-            freq_x = jnp.where(lane < 64, lane, lane - LANES)
-            freq_y = jnp.full((NG, LANES), signed(me * ROWS + r), jnp.int32)
+        if r < ROWS - 1:
+            near = me * (ROWS - 1) + r
+            freq_x = signed_kx(lane // 32, lax.rem(lane, 32))
+            freq_y = jnp.full((NG, LANES), signed(jnp.where(near < 64, near, near + 32)), jnp.int32)
             held = mask[pl.ds(r, 1), pl.ds(0, LANES)]
+        elif r < ROWS:
+            freq_x = jnp.where(lent(me, lane // 32), outer_x, signed_kx(lane // 32, lax.rem(lane, 32)))
+            freq_y = jnp.where(lent(me, lane // 32), outer_y, signed(64 + me))
+            held = jnp.where(lent(me, quad), outer_held, mask[pl.ds(r, 1), pl.ds(0, LANES)])
         else:
-            freq_x = signed(64 + lax.rem(lane, 32))
-            freq_y = me * QUADS + lane // 32 - 64
-            held = jnp.zeros((1, LANES), jnp.float32)
-            for e in range(QUADS):
-                held = jnp.where(quad == e, mask[pl.ds(8 + e, 1), pl.ds(LANES, LANES)], held)
+            freq_x, freq_y = outer_x, outer_y
+            held = jnp.where(quad < 2, outer_held, 0.0)
         inside = freq_x * freq_x + freq_y * freq_y + freq_z * freq_z <= (NG // 2) * (NG // 2)
         wave_x = freq_x.astype(jnp.float32) + q[0:1]
         wave_y = freq_y.astype(jnp.float32) + q[1:2]
@@ -202,18 +236,16 @@
         weights[:, pl.ds(LANES * r, LANES)] = jnp.where(inside & (held > 0.5), weight, 0.0)
 
     wx[...] = jnp.zeros_like(wx)
-    row_i = lax.broadcasted_iota(jnp.int32, (256, 256), 0)
-    col_i = lax.broadcasted_iota(jnp.int32, (256, 256), 1)
-    for b in range(FOLD):
-        move = jnp.where(col_i == row_i + 32 * b, 1.0, 0.0).astype(jnp.bfloat16)
-        for p in range(2):
-            wx[b, pl.ds(256 * p + 32 * b, NG), :] = fx[pl.ds(NG * p, NG), :]
-            wb[b, :, pl.ds(256 * p, 256)] = dot(bx[:, pl.ds(256 * p, 256)], move).astype(jnp.bfloat16)
+    for p in range(2):
+        wx[pl.ds(256 * p, NG), :] = fx[pl.ds(NG * p, NG), :]
 
     lane_quad = lax.broadcasted_iota(jnp.int32, (2 * NG, LANES), 1) // 32
 
-    def row_of(z):
-        return 2 * GROUPS * z + 4 * (z // 3)
+    small_lane = lax.broadcasted_iota(jnp.int32, (FFT, LANES), 1)
+    small_lent = lent(lax.broadcasted_iota(jnp.int32, (FFT, LANES), 0), small_lane // 32)
+
+    def joined(real, imaginary):
+        return jnp.where(small_lane < HALF, real, pltpu.roll(imaginary, HALF, axis=1))
 
     def block_to(peer, send, recv, send_sem, recv_sem):
         return pltpu.make_async_remote_copy(
@@ -222,8 +254,8 @@
             device_id=(pool, peer), device_id_type=mesh_id,
         )
 
-    def post(step, send, recv, send_sem, recv_sem):
-        rows = slice(OFFSETS[step], OFFSETS[step] + PIECE * STEPS[step][1])
+    def post(rows, send, recv, send_sem, recv_sem):
+        rows = slice(rows[0], rows[0] + rows[1])
         send[...] = stage[...].reshape(FFT, PITCH, LANES)[:, rows].astype(jnp.bfloat16)
 
         def start(k, carry):
@@ -240,12 +272,12 @@
             device_id=(after, me), device_id_type=mesh_id,
         )
 
-    def collect(step, send, recv, send_sem, recv_sem):
+    def collect(rows, send, recv, send_sem, recv_sem):
         others(send, recv, send_sem, recv_sem).wait_recv()
 
         def spread(d, carry):
-            start = pl.multiple_of(d * PITCH + OFFSETS[step], 8)
-            stage[pl.ds(start, PIECE * STEPS[step][1]), :] = recv[d].astype(jnp.float32)
+            start = pl.multiple_of(d * PITCH + rows[0], 8)
+            stage[pl.ds(start, rows[1]), :] = recv[d].astype(jnp.float32)
             return carry
 
         lax.fori_loop(0, FFT, spread, 0, unroll=4)
@@ -264,63 +296,92 @@
         for t in range(TILES):
             own_re, own_im = halves(flat_a, t)
             rec_re, rec_im = halves(flat_b, t)
-            den_re.append((rec_re * own_re + rec_im * own_im).astype(jnp.bfloat16))
-            den_im.append((rec_re * own_im - rec_im * own_re).astype(jnp.bfloat16))
+            den_re.append(rec_re * own_re + rec_im * own_im)
+            den_im.append(rec_re * own_im - rec_im * own_re)
+        runs = []
         for b in range(FOLD):
-            cells = jnp.concatenate(den_re[b : b + 2] + den_im[b : b + 2], axis=1)
-            along = dot(cells, wx[b])
-            for p in range(2):
-                t_main[pl.ds(NG * p + DEEP * b, DEEP), :] = along[:, LANES * p : LANES * (p + 1)]
-                t_edge[pl.ds(NG * p + DEEP * b, DEEP), :] = along[:, LANES * (2 + p) : LANES * (3 + p)]
-        made = dot(fym[...], t_main[...].astype(jnp.bfloat16))
-        side = t_edge[...]
+            parts = [jnp.concatenate(den[b : b + 2], axis=1) for den in (den_re, den_im)]
+            if b > 0:
+                parts = [pltpu.roll(part, 256 - 32 * b, axis=1) for part in parts]
+            runs.append(jnp.concatenate(parts, axis=1))
+        along = dot(jnp.concatenate(runs, axis=0).astype(jnp.bfloat16), wx[...])
+        planes = [along[:, LANES * k : LANES * (k + 1)] for k in range(4)]
+        made = dot(fym[...], jnp.concatenate(planes[:2], axis=0).astype(jnp.bfloat16))
+        side = jnp.concatenate(planes[2:], axis=0)
         quads = [jnp.where(lane_quad == e, side, 0.0).astype(jnp.bfloat16) for e in range(QUADS)]
         edge = dot(fye[...], jnp.concatenate(quads, axis=0))
-        for r in range(GROUPS):
+        edges = [edge[p * FFT : (p + 1) * FFT] for p in range(2)]
+        for r in range(ROWS):
             for p in range(2):
-                piece = made[(2 * r + p) * FFT : (2 * r + p + 1) * FFT] if r < ROWS else edge[p * FFT : (p + 1) * FFT]
-                stage[pl.ds(row_of(z) + 2 * r + p, FFT, stride=PITCH), :] = piece
+                piece = made[(2 * r + p) * FFT : (2 * r + p + 1) * FFT]
+                if r == ROWS - 1:
+                    piece = jnp.where(small_lent, edges[p], piece)
+                stage[pl.ds(SHARE * z + 2 * r + p, FFT, stride=PITCH), :] = piece
+        stage[pl.ds(SHARE * z + 2 * ROWS, FFT, stride=PITCH), :] = joined(*edges)
         return carry
 
-    for step, (first, count_z) in enumerate(STEPS):
-        lax.fori_loop(first, first + count_z, forward, 0)
-        post(step, *out_legs[step])
+    lax.fori_loop(0, 3, forward, 0)
+
+    @pl.when(pool < LATE)
+    def _():
+        post(OUT_ROWS[0], *out_legs[0])
+
+    lax.fori_loop(3, PLANES, forward, 0)
+
+    @pl.when(pool >= LATE)
+    def _():
+        post(OUT_ROWS[0], *out_legs[0])
+
+    post(OUT_ROWS[1], *out_legs[1])
 
     for step in range(2):
-        collect(step, *out_legs[step])
-    for r in range(GROUPS):
-        runs = [stage[pl.ds(row_of(z) + 2 * r + p, FFT, stride=PITCH), :] for z in range(PLANES) for p in range(2)]
-        spectrum = dot(fz[...], jnp.concatenate(runs, axis=0).astype(jnp.bfloat16))
-        weight = weights[:, pl.ds(LANES * r, LANES)]
-        for p in range(2):
-            scaled[pl.ds(NG * p, NG), pl.ds(LANES * r, LANES)] = (spectrum[NG * p : NG * (p + 1)] * weight).astype(jnp.bfloat16)
-
-    def give_back(z, carry):
-        returned = dot(bz[pl.ds(pl.multiple_of(z * 2 * FFT, 2 * FFT), 2 * FFT), :], scaled[...])
-        for r in range(GROUPS):
-            for p in range(2):
-                piece = returned[p * FFT : (p + 1) * FFT, LANES * r : LANES * (r + 1)]
-                stage[pl.ds(row_of(z) + 2 * r + p, FFT, stride=PITCH), :] = piece
-        return carry
-
-    for step, (first, count_z) in enumerate(STEPS):
-        lax.fori_loop(first, first + count_z, give_back, 0)
-        post(step, *back_legs[step])
+        collect(OUT_ROWS[step], *out_legs[step])
+    for first in range(0, GROUPS, 2):
+        fields = []
+        for r in (first, first + 1):
+            if r < ROWS:
+                runs = [stage[pl.ds(SHARE * z + 2 * r + p, FFT, stride=PITCH), :] for z in range(PLANES) for p in range(2)]
+            else:
+                both = [stage[pl.ds(SHARE * z + 2 * ROWS, FFT, stride=PITCH), :] for z in range(PLANES)]
+                runs = [part for row in both for part in (row, pltpu.roll(row, HALF, axis=1))]
+            fields.append(jnp.concatenate(runs, axis=0))
+        spectrum = dot(fz[...], jnp.concatenate(fields, axis=1).astype(jnp.bfloat16))
+        weight = weights[:, pl.ds(LANES * first, 2 * LANES)]
+        scaled = jnp.concatenate([spectrum[:NG] * weight, spectrum[NG:] * weight], axis=0).astype(jnp.bfloat16)
+        returned = dot(bz[...], scaled)
+        for r in (first, first + 1):
+            part = returned[:, LANES * (r - first) : LANES * (r - first + 1)]
+            for z in range(PLANES):
+                pair = [part[FFT * (2 * z + p) : FFT * (2 * z + p + 1)] for p in range(2)]
+                if r < ROWS:
+                    for p in range(2):
+                        stage[pl.ds(SHARE * z + 2 * r + p, FFT, stride=PITCH), :] = pair[p]
+                else:
+                    stage[pl.ds(SHARE * z + 2 * ROWS, FFT, stride=PITCH), :] = joined(*pair)
+
+    post(BACK_ROWS[0], *back_legs[0])
+    post(BACK_ROWS[1], *back_legs[1])
 
     def inverse(z, carry):
         flat_b[...] = rec[z].astype(jnp.float32)
-        base = row_of(z)
-        runs = [stage[pl.ds(base + i, FFT, stride=PITCH), :] for i in range(PIECE)]
-        main = jnp.concatenate(runs[: 2 * ROWS], axis=0)
-        edge = jnp.concatenate(runs[2 * ROWS :], axis=0)
+        runs = [stage[pl.ds(SHARE * z + i, FFT, stride=PITCH), :] for i in range(SHARE)]
+        half_row = (runs[2 * ROWS], pltpu.roll(runs[2 * ROWS], HALF, axis=1))
+        last = runs[2 * ROWS - 2 : 2 * ROWS]
+        kept = [jnp.where(small_lent, 0.0, row) for row in last]
+        main = jnp.concatenate(runs[: 2 * ROWS - 2] + kept, axis=0)
+        edge = [jnp.where(small_lane < HALF, half_row[p], jnp.where(small_lent, last[p], 0.0)) for p in range(2)]
+        edge = jnp.concatenate(edge, axis=0)
         quads = lane_quad[: 2 * FFT]
         edges = jnp.concatenate([jnp.where(quads == e, edge, 0.0) for e in range(QUADS)], axis=0)
-        t_main[...] = dot(bym[...], main.astype(jnp.bfloat16))
-        t_edge[...] = dot(bye[...], edges.astype(jnp.bfloat16))
+        columns = [dot(bym[...], main.astype(jnp.bfloat16)), dot(bye[...], edges.astype(jnp.bfloat16))]
+        parts = [column[NG * p : NG * (p + 1)] for column in columns for p in range(2)]
+        along = dot(jnp.concatenate(parts, axis=1).astype(jnp.bfloat16), bx[...])
         shares = []
         for b in range(FOLD):
-            parts = [t[pl.ds(NG * p + DEEP * b, DEEP), :] for t in (t_main, t_edge) for p in range(2)]
-            shares.append(dot(jnp.concatenate(parts, axis=1).astype(jnp.bfloat16), wb[b]))
+            windows = [along[DEEP * b : DEEP * (b + 1), 256 * p : 256 * (p + 1)] for p in range(2)]
+            if b > 0:
+                windows = [pltpu.roll(window, 32 * b, axis=1) for window in windows]
+            shares.append(jnp.concatenate(windows, axis=1))
         for t in range(TILES):
             field = []
             for p in range(2):
@@ -337,9 +398,10 @@
         out[z] = flat_a[...].astype(jnp.bfloat16)
         return carry
 
-    for step, (first, count_z) in enumerate(STEPS):
-        collect(step, *back_legs[step])
-        lax.fori_loop(first, first + count_z, inverse, 0)
+    collect(BACK_ROWS[0], *back_legs[0])
+    lax.fori_loop(0, 3, inverse, 0)
+    collect(BACK_ROWS[1], *back_legs[1])
+    lax.fori_loop(3, PLANES, inverse, 0)
 
     for z in range(PLANES):
         shift(z).wait_send()
@@ -368,19 +430,15 @@
         ]
         + [pltpu.VMEM(t.shape, bf16) for t in constants]
         + [
-            pltpu.VMEM((FOLD, 512, 512), bf16),
-            pltpu.VMEM((FOLD, 512, 512), bf16),
+            pltpu.VMEM((512, 512), bf16),
             pltpu.VMEM(orb.shape, bf16),
             pltpu.VMEM((RAW, LANES), f32),
             pltpu.VMEM((RAW, LANES), f32),
-            pltpu.VMEM((2 * NG, LANES), f32),
-            pltpu.VMEM((2 * NG, LANES), f32),
             pltpu.VMEM((FFT * PITCH, LANES), f32),
             pltpu.VMEM((NG, GROUPS * LANES), f32),
-            pltpu.VMEM((2 * NG, GROUPS * LANES), bf16),
             pltpu.VMEM((16, 2 * LANES), f32),
         ]
-        + [pltpu.VMEM((FFT, PIECE * n, LANES), bf16) for _, n in STEPS for _ in range(4)]
+        + [pltpu.VMEM((FFT, rows[k][1], LANES), bf16) for k in range(2) for rows in (OUT_ROWS, OUT_ROWS, BACK_ROWS, BACK_ROWS)]
         + [
             pltpu.SemaphoreType.DMA((3 + len(constants),)),
             pltpu.SemaphoreType.DMA((PLANES,)),

time: 66.9 us -> 65.4 us (0.978)
  Pallas kernels: 66 us -> 64.4 us
    pallas_call x1, Pallas kernels: 66 us -> 64.4 us  [local(): pl.pallas_call(kernel, name='exchange_step', out_shape=jax.ShapeDtypeStru...]
where the time goes in v5:
time: 65.4 us; the launch traced here: 65.2 us
  Pallas kernels  64.4 us (98%)
  local copies, waits for them, and re-layouts  0.79 us (1%)
    pallas_call x1, Pallas kernels, local(): pl.pallas_call(kernel, name='exchange_step', out_shape=jax.ShapeDtypeStru...  64.4 us

profile of v5, /device:TPU:1, one launch (start us, length us, event | category | flops | bytes accessed | tf_op | source)
XLA Modules:
  0.0 65.2 jit_solution(1778263070213096567)
XLA Ops:
  0.0 64.4 %exchange_step.1 = bf16[5,400,128]{2,1,0:T(8,128)(2,1)S(1)} custom-call(s32[3,16]{1,0:T(4,128)} %bitcast.15, bf16[5,400,128]{2,1,0:T(8,128)(2,1)} %bitcast.13, s32[125,128]{1,0:T(8,128)} %bitcast.14, bf16[320,512]{1,0:T(8,128)(2,1)} %constant.16.clone.fx_h, bf16[320,320]{1,0:T(8,128)(2,1)} %constant.17.clone.fym_h, bf16[64,1280]{1,0:T(8,128)(2,1)} %constant.18.clone.fye_h, ...), custom_call_target="tpu_custom_call" | custom-call | tf_op jit(solution)/shard_map/exchange_step/pallas_call | solution.py:420
  64.4 0.8 %copy.15 = bf16[1,2,1,5,25600]{4,1,3,2,0:T(2,128)(2,1)} copy(bf16[1,2,1,5,25600]{4,1,3,2,0:T(2,128)(2,1)S(1)} %bitcast.12) | data formatting | bytes 1024000

commit v6 on v5

--- a/solution.py
+++ b/solution.py
@@ -247,6 +247,10 @@
     def joined(real, imaginary):
         return jnp.where(small_lane < HALF, real, pltpu.roll(imaginary, HALF, axis=1))
 
+    def partner(code):
+        bits = [(lax.rem(me // (1 << i), 2), lax.rem(code // (1 << i), 2)) for i in range(5)]
+        return sum((1 << i) * (mine + other - 2 * mine * other) for i, (mine, other) in enumerate(bits))
+
     def block_to(peer, send, recv, send_sem, recv_sem):
         return pltpu.make_async_remote_copy(
             src_ref=send.at[peer], dst_ref=recv.at[me],
@@ -259,7 +263,7 @@
         send[...] = stage[...].reshape(FFT, PITCH, LANES)[:, rows].astype(jnp.bfloat16)
 
         def start(k, carry):
-            block_to(lax.rem(me + k, FFT), send, recv, send_sem, recv_sem).start()
+            block_to(partner(FFT - k), send, recv, send_sem, recv_sem).start()
             return carry
 
         lax.fori_loop(1, FFT, start, 0)
@@ -322,13 +326,13 @@
 
     lax.fori_loop(0, 3, forward, 0)
 
-    @pl.when(pool < LATE)
+    @pl.when((pool < LATE) & (pool != 1))
     def _():
         post(OUT_ROWS[0], *out_legs[0])
 
     lax.fori_loop(3, PLANES, forward, 0)
 
-    @pl.when(pool >= LATE)
+    @pl.when((pool >= LATE) | (pool == 1))
     def _():
         post(OUT_ROWS[0], *out_legs[0])
 

time: 65.4 us -> 65.3 us (level)
  no operation moved by 1% of the time
where the time goes in v6:
time: 65.3 us; the launch traced here: 65.1 us
  Pallas kernels  64.3 us (98%)
  local copies, waits for them, and re-layouts  0.79 us (1%)
    pallas_call x1, Pallas kernels, local(): pl.pallas_call(kernel, name='exchange_step', out_shape=jax.ShapeDtypeStru...  64.3 us

profile of v6, /device:TPU:1, one launch (start us, length us, event | category | flops | bytes accessed | tf_op | source)
XLA Modules:
  0.0 65.1 jit_solution(12782729265019088184)
XLA Ops:
  0.0 64.3 %exchange_step.1 = bf16[5,400,128]{2,1,0:T(8,128)(2,1)S(1)} custom-call(s32[3,16]{1,0:T(4,128)} %bitcast.15, bf16[5,400,128]{2,1,0:T(8,128)(2,1)} %bitcast.13, s32[125,128]{1,0:T(8,128)} %bitcast.14, bf16[320,512]{1,0:T(8,128)(2,1)} %constant.16.clone.fx_h, bf16[320,320]{1,0:T(8,128)(2,1)} %constant.17.clone.fym_h, bf16[64,1280]{1,0:T(8,128)(2,1)} %constant.18.clone.fye_h, ...), custom_call_target="tpu_custom_call" | custom-call | tf_op jit(solution)/shard_map/exchange_step/pallas_call | solution.py:424
  64.3 0.8 %copy.15 = bf16[1,2,1,5,25600]{4,1,3,2,0:T(2,128)(2,1)} copy(bf16[1,2,1,5,25600]{4,1,3,2,0:T(2,128)(2,1)S(1)} %bitcast.12) | data formatting | bytes 1024000
